TPU v7x, 32 devices: a whole 2x2x4 slice. The times are simulated.
32 devices in a mesh: leaf: 8 (over z, x), sub: 4 (over y, core).
Axes of the slice: x: 2, y: 2, z: 4, core: 2. Of those that a mesh axis runs over, the one named last changes fastest.
Arguments:
- vectors: bfloat16 [64, 163840], P(None, ('leaf', 'sub')), may hold values from -6 to 6
- row_counts: int32 [32], replicated, may hold values from 3072 to 5120, as said below
- tree_slot: int32 [163840], P(('leaf', 'sub')), may hold values from -1 to 131071, as said below
- leaf_inverse: bfloat16 [512, 256, 256], P(('leaf', 'sub')), may hold values from -0.375 to 0.375
- left_basis: bfloat16 [9, 32, 131072], P(None, None, ('leaf', 'sub')), may hold values from -0.41992188 to 0.41992188
- right_basis: bfloat16 [9, 32, 131072], P(None, None, ('leaf', 'sub')), may hold values from -6 to 6
Outputs:
- applied: bfloat16 [64, 163840], P(None, ('leaf', 'sub'))
Inputs may be any that keep to these rules, and one draw needn't show every extreme that they name: The first row_counts[d] of the 5120 slots of owner d are live; the counts sum to 131072. `tree_slot`: live slots hold distinct tree positions covering 0 .. 131071, dead slots hold -1. Tree owner t holds positions t*4096 .. (t+1)*4096 - 1; the live rows of one mesh owner go to one tree owner at most 160 at a time.
All inputs are finite; a program needn't handle non-finite values.
Results may differ from a plain program's by a relative error of at most 0.014.
Values may be sent and summed in bfloat16 or wider, within the bound.
No kernel may reach another device: no remote copies, remote signals or barrier semaphores. Data moves between devices by JAX's collectives and lax.ppermute only.
A program may use at most 64 MiB of HBM per device.

v0:
```python
import functools
import math

import jax
import jax.numpy as jnp
from jax import lax
from jax.experimental import pallas as pl
from jax.experimental.pallas import tpu as pltpu
from jax.sharding import PartitionSpec as P

F32 = jnp.float32
BF16 = jnp.bfloat16
I32 = jnp.int32
LANES = 128
DIGIT = 64
NT = (((1,), (1,)), ((), ()))
VMEM = pltpu.VMEM
SMEM = pltpu.SMEM
CHUNKS = 1


def dot(a, b):
    return jnp.dot(a, b, preferred_element_type=F32)


def dot_nt(a, b):
    return lax.dot_general(a, b, NT, preferred_element_type=F32)


def iota(shape, dim):
    return lax.broadcasted_iota(I32, shape, dim)


def rows_at(start, size):
    return pl.ds(pl.multiple_of(start, 8), size)


def send_kernel(rows, vecs, chunks, half, n_sub, counts_ref, vec_ref, slot_ref, *refs):
    outs = refs[:chunks]
    row_ref, part_ref, xt, staged, flat, places, posf, sem = refs[chunks:]
    devices = outs[0].shape[0]
    width = vecs // chunks
    parts = LANES // width
    blocks = slot_ref.shape[0]
    count = counts_ref[lax.axis_index("leaf") * n_sub + lax.axis_index("sub")]
    trash = devices * parts * half
    shift = rows.bit_length() - 1
    owner_id = iota((devices, LANES), 0)
    before = (iota((LANES, LANES), 0) < iota((LANES, LANES), 1)).astype(BF16)
    ones = jnp.ones((LANES, LANES), BF16)
    code_id = iota((parts * LANES, LANES), 0)
    carry = jnp.zeros((devices, LANES), F32)
    pos = jnp.zeros((2 * devices, parts * LANES), F32)
    for b in range(blocks):
        slot = slot_ref[b : b + 1, :]
        lane = iota((1, LANES), 1) + b * LANES
        live = (lane < count) & (slot >= 0)
        owner = jnp.where(live, slot >> shift, -1)
        local = slot & (rows - 1)
        hot = owner_id == owner
        hot_b = jnp.where(hot, 1.0, 0.0).astype(BF16)
        ranks = dot(hot_b, before) + carry
        carry = carry + dot(hot_b, ones)
        rank = jnp.sum(jnp.where(hot, ranks, 0.0), axis=0, keepdims=True).astype(I32)
        flat[b : b + 1, :] = jnp.where(live, owner * (parts * half) + rank, trash)
        part = jnp.zeros((1, LANES), I32)
        for q in range(1, parts):
            part = part + jnp.where(rank >= q * half, 1, 0)
        inner = rank - part * half
        row_ref[b : b + 1, :] = jnp.where(live, owner * half + inner, 0)
        part_ref[b : b + 1, :] = jnp.where(live, part, parts)
        high = ((local >> 6) + 1).astype(F32)
        low = (local & (DIGIT - 1)).astype(F32)
        digits = jnp.concatenate(
            [jnp.where(hot, high, 0.0), jnp.where(hot, low, 0.0)], axis=0
        ).astype(BF16)
        spread = jnp.where(code_id == part * LANES + inner, 1.0, 0.0).astype(BF16)
        pos = pos + dot_nt(digits, spread)
    copy = pltpu.make_async_copy(flat, places, sem)
    copy.start()
    for d in range(devices):
        for q in range(parts):
            at = slice(q * LANES, (q + 1) * LANES)
            posf[8 * d + q : 8 * d + q + 1, :] = pos[d : d + 1, at]
            posf[8 * d + parts + q : 8 * d + parts + q + 1, :] = pos[devices + d : devices + d + 1, at]

    def turn(b, _):
        x = vec_ref[:, pl.ds(pl.multiple_of(b * LANES, LANES), LANES)].astype(F32)
        xt[rows_at(b * LANES, LANES), :] = jnp.concatenate([x, x], axis=0).T
        return 0

    lax.fori_loop(0, blocks, turn, 0, unroll=8)
    copy.wait()

    def move(b, _):
        for u in range(LANES):
            staged[pl.ds(places[b, u], 1), :] = xt[pl.ds(b * LANES + u, 1), :]
        return 0

    lax.fori_loop(0, blocks, move, 0)
    group = iota((half, LANES), 1) // width

    def pack(d, _):
        direct = [staged[rows_at((d * parts + q) * half, half), :] for q in range(parts)]
        moved = [pltpu.roll(x, width, 1) for x in direct] if chunks == 2 else direct
        for c in range(chunks):
            packed = None
            for q in range(parts):
                x = direct[q] if q % chunks == c else moved[q]
                packed = x if packed is None else jnp.where(group == q, x, packed)
            outs[c][d, pl.ds(0, half), :] = packed.astype(BF16)
        outs[0][d, pl.ds(half, 8), :] = posf[rows_at(d * 8, 8), :].astype(BF16)
        return 0

    lax.fori_loop(0, devices, pack, 0)


def band_tiles(halves, levels):
    tiles = [("b", h, k) for k in range(levels) for h in range(halves)]
    return tiles + [("g", j, k) for j in range(levels) for k in range(j + 1, levels)]


def band_rows(halves, levels, rank):
    return (len(band_tiles(halves, levels)) + 3) // 4 * rank


def pack_bands(ref, b, gram, rank, halves, levels):
    tiles = band_tiles(halves, levels)
    blank = jnp.zeros((rank, rank), F32)
    for r in range(0, len(tiles), 4):
        band = []
        for kind, x, k in tiles[r : r + 4]:
            at = slice(k * rank, (k + 1) * rank)
            band.append(b[x * rank : (x + 1) * rank, at] if kind == "b" else gram[x][:, at])
        band += [blank] * (4 - len(band))
        ref[r // 4 * rank : (r // 4 + 1) * rank, :] = jnp.concatenate(band, axis=1).astype(BF16)


def unpack_bands(value, rank, halves, levels):
    tiles = band_tiles(halves, levels)
    found = {}
    for t, key in enumerate(tiles):
        found[key] = value[t // 4 * rank : (t // 4 + 1) * rank, t % 4 * rank : (t % 4 + 1) * rank]
    b = jnp.concatenate(
        [
            jnp.concatenate([found["b", h, k] for k in range(levels)], axis=1)
            for h in range(halves)
        ],
        axis=0,
    )
    blank = jnp.zeros((rank, rank), F32)
    gram = [
        jnp.concatenate([found["g", j, k] if k > j else blank for k in range(levels)], axis=1)
        for j in range(levels)
    ]
    return b, gram


def tree_kernel(
    local_levels, leaf, rank, arr_ref, pos_ref, inv, left, right, gram_ref,
    field_ref, message_ref, spot_ref, arr, tree, spots, sem,
):
    devices = arr_ref.shape[0]
    vecs, rows = field_ref.shape
    parts = LANES // vecs
    half = arr.shape[0] // devices
    leaves = rows // leaf
    levels = right.shape[0]
    for d in range(devices):
        pos = pos_ref[d, half : half + 8, :].astype(F32)
        high = pos[0:parts, :]
        low = pos[parts : 2 * parts, :]
        spot = jnp.where(high > 0.5, (high - 1.0) * DIGIT + low, float(rows)).astype(I32)
        spot_ref[parts * d : parts * (d + 1), :] = spot
    copy = pltpu.make_async_copy(spot_ref, spots, sem)
    copy.start()

    def widen(d, _):
        arr[rows_at(d * half, half), :] = arr_ref[d, pl.ds(0, half), :].astype(F32)
        return 0

    lax.fori_loop(0, devices, widen, 0)

    def clear(i, _):
        tree[rows_at(i * 128, 128), :] = jnp.zeros((128, LANES), F32)
        return 0

    lax.fori_loop(0, rows // 128, clear, 0)
    copy.wait()

    def place(d, _):
        for u in range(half):
            row = arr[pl.ds(d * half + u, 1), :]
            for q in range(parts):
                at = pl.ds(spots[parts * d + q, u], 1)
                tree[at, pl.ds(q * vecs, vecs)] = row[:, q * vecs : (q + 1) * vecs]
        return 0

    lax.fori_loop(0, devices, place, 0)
    for l in range(leaves):
        block = tree[l * leaf : (l + 1) * leaf, :].astype(BF16)
        turned = dot(inv[l], block).T
        total = turned[:vecs]
        for q in range(1, parts):
            total = total + turned[q * vecs : (q + 1) * vecs]
        field_ref[:, l * leaf : (l + 1) * leaf] = total
    for k in range(local_levels):
        size = leaf << k
        scale = 1.0 / math.sqrt(size)
        coeff = []
        for n in range(rows // size):
            at = slice(n * size, (n + 1) * size)
            part = dot_nt(field_ref[:, at].astype(BF16), right[k, :, at])
            coeff.append((part * scale).astype(BF16))
        for n in range(rows // size):
            at = slice(n * size, (n + 1) * size)
            field_ref[:, at] = field_ref[:, at] - dot(coeff[n ^ 1], left[k, :, at])
    rounded = field_ref[...].astype(BF16)
    cross = levels - local_levels
    b = jnp.concatenate([dot_nt(rounded, right[k]) for k in range(local_levels, levels)], axis=1)
    gram = [gram_ref[j * rank : (j + 1) * rank, :] for j in range(cross)]
    pack_bands(message_ref, b, gram, rank, vecs // rank, cross)


def gram_kernel(first, left, right, out_ref):
    levels = left.shape[0]
    lhs = jnp.concatenate([left[k] for k in range(first, levels)], axis=0)
    rhs = jnp.concatenate([right[k] for k in range(first, levels)], axis=0)
    out_ref[...] = dot_nt(lhs, rhs)


def merge_kernel(bits, rank, scales, vecs, levels, *refs):
    group = 1 << bits
    p_ref = refs[group]
    halves = vecs // rank
    found = [unpack_bands(r[...].astype(F32), rank, halves, levels) for r in refs[:group]]
    b = [f[0] for f in found]
    gram = [f[1] for f in found]
    for step in range(bits):
        at = slice(step * rank, (step + 1) * rank)
        p = [(b[x ^ 1][:, at] * scales[step]).astype(BF16) for x in range(len(b))]
        p_ref[:, at] = p[0]
        if step + 1 < levels:
            b = [b[x] - dot(p[x], gram[x][step].astype(BF16)) for x in range(len(b))]
            b = [b[x] + b[x + 1] for x in range(0, len(b), 2)]
            gram = [
                [u + v for u, v in zip(gram[x], gram[x + 1])] for x in range(0, len(gram), 2)
            ]
    if levels > bits:
        keep = slice(bits * rank, levels * rank)
        rest = [g[:, keep] for g in gram[0][bits:]]
        pack_bands(refs[group + 1], b[0][:, keep], rest, rank, halves, levels - bits)


def back_kernel(first, rank, n_solved, field_ref, left, spot_ref, *refs):
    solved = refs[:n_solved]
    out_ref, done, spots, packed, sem = refs[n_solved:]
    devices, half, _ = out_ref.shape
    vecs, rows = field_ref.shape
    parts = LANES // vecs
    levels = left.shape[0]
    copy = pltpu.make_async_copy(spot_ref, spots, sem)
    copy.start()
    p = jnp.concatenate([r[...] for r in solved], axis=1)
    wide = 512
    for c in range(rows // wide):
        at = slice(c * wide, (c + 1) * wide)
        basis = jnp.concatenate([left[k, :, at] for k in range(first, levels)], axis=0)
        field = field_ref[:, at] - dot(p, basis)
        for q in range(wide // LANES):
            x = field[:, q * LANES : (q + 1) * LANES]
            low = c * wide + q * LANES
            done[low : low + LANES, :] = jnp.concatenate([x] * parts, axis=0).T
    copy.wait()
    group = iota((1, LANES), 1) // vecs

    def pick(d, _):
        for u in range(half):
            row = done[pl.ds(spots[parts * d, u], 1), :]
            for q in range(1, parts):
                row = jnp.where(group == q, done[pl.ds(spots[parts * d + q, u], 1), :], row)
            packed[pl.ds(d * half + u, 1), :] = row
        return 0

    lax.fori_loop(0, devices, pick, 0)

    def narrow(d, _):
        out_ref[d, :, :] = packed[rows_at(d * half, half), :].astype(BF16)
        return 0

    lax.fori_loop(0, devices, narrow, 0)


def final_kernel(ret_ref, row_ref, part_ref, out_ref, ret, picked, places, sem):
    devices, half, _ = ret_ref.shape
    vecs = out_ref.shape[0]
    parts = LANES // vecs
    blocks = row_ref.shape[0]
    copy = pltpu.make_async_copy(row_ref, places, sem)
    copy.start()

    def widen(d, _):
        ret[rows_at(d * half, half), :] = ret_ref[d, :, :].astype(F32)
        return 0

    lax.fori_loop(0, devices, widen, 0)
    copy.wait()

    def move(b, _):
        for u in range(LANES):
            picked[pl.ds(b * LANES + u, 1), :] = ret[pl.ds(places[b, u], 1), :]
        return 0

    lax.fori_loop(0, blocks, move, 0)
    for b in range(blocks):
        x = picked[b * LANES : (b + 1) * LANES, :].T
        part = part_ref[b : b + 1, :]
        value = jnp.zeros((vecs, LANES), F32)
        for q in range(parts):
            value = jnp.where(part == q, x[q * vecs : (q + 1) * vecs], value)
        out_ref[:, b * LANES : (b + 1) * LANES] = value.astype(BF16)


def full(shape, dtype):
    return jax.ShapeDtypeStruct(shape, dtype)


def vmem():
    return pl.BlockSpec(memory_space=VMEM)


def call(kernel, name, mib, flops, out_shape, in_specs, out_specs, scratch_shapes=()):
    return pl.pallas_call(
        kernel,
        out_shape=out_shape,
        in_specs=in_specs,
        out_specs=out_specs,
        scratch_shapes=scratch_shapes,
        compiler_params=pltpu.CompilerParams(vmem_limit_bytes=mib << 20),
        cost_estimate=pl.CostEstimate(flops=flops, bytes_accessed=1 << 20, transcendentals=0),
        name=name,
    )


def flipped(block, axis, mask):
    count = lax.axis_size(axis)
    return lax.ppermute(block, axis, [(i, i ^ mask) for i in range(count)])


def body(vectors, row_counts, tree_slot, leaf_inverse, left_basis, right_basis):
    vecs, slots = vectors.shape
    leaves, leaf = leaf_inverse.shape[0], leaf_inverse.shape[1]
    rows = leaves * leaf
    levels, rank = left_basis.shape[0], left_basis.shape[1]
    n_leaf = lax.axis_size("leaf")
    n_sub = lax.axis_size("sub")
    devices = n_leaf * n_sub
    sub_bits = n_sub.bit_length() - 1
    leaf_bits = n_leaf.bit_length() - 1
    cross = sub_bits + leaf_bits
    local_levels = levels - cross
    cap = (slots + devices - 1) // devices
    blocks = slots // LANES
    axes = ("leaf", "sub")
    chunks = CHUNKS
    width = vecs // chunks
    parts = LANES // width
    half = ((cap + parts - 1) // parts + 7) // 8 * 8
    if vecs * 2 != LANES or half > LANES or slots % LANES or rows & (rows - 1):
        raise ValueError("unsupported sizes")

    smem = pl.BlockSpec(memory_space=SMEM)
    outgoing = call(
        functools.partial(send_kernel, rows, vecs, chunks, half, n_sub),
        "send",
        20,
        1 << 30,
        tuple(
            full((devices, half + 8 if c == 0 else half, LANES), BF16) for c in range(chunks)
        )
        + (full((blocks, LANES), I32), full((blocks, LANES), I32)),
        [smem, vmem(), vmem()],
        (vmem(),) * (chunks + 2),
        [
            VMEM((slots, LANES), F32),
            VMEM((devices * parts * half + 8, LANES), F32),
            VMEM((blocks, LANES), I32),
            SMEM((blocks, LANES), I32),
            VMEM((8 * devices, LANES), F32),
            pltpu.SemaphoreType.DMA,
        ],
    )(row_counts, vectors, tree_slot.reshape(blocks, LANES))
    row_of, part_of = outgoing[chunks:]

    def exchange(x):
        return lax.all_to_all(x, axes, split_axis=0, concat_axis=0, tiled=True)

    arrived = [exchange(x) for x in outgoing[:chunks]]

    gram = call(
        functools.partial(gram_kernel, local_levels),
        "gram",
        8,
        1 << 30,
        full((cross * rank, cross * rank), F32),
        [vmem(), vmem()],
        vmem(),
    )(left_basis, right_basis)

    stages = []
    for axis, n_bits in (("sub", sub_bits), ("leaf", leaf_bits)):
        bit = 0
        while bit < n_bits:
            take = min(2, n_bits - bit)
            stages.append((axis, bit, take))
            bit += take
    halves = width // rank
    results = []
    for c in range(chunks):
        field, message, spots = call(
            functools.partial(tree_kernel, local_levels, leaf, rank),
            "tree",
            20,
            1 << 30,
            (
                full((width, rows), F32),
                full((band_rows(halves, cross, rank), LANES), BF16),
                full((parts * devices, LANES), I32),
            ),
            [vmem()] * 6,
            (vmem(), vmem(), vmem()),
            [
                VMEM((devices * half, LANES), F32),
                VMEM((rows + 8, LANES), F32),
                SMEM((parts * devices, LANES), I32),
                pltpu.SemaphoreType.DMA,
            ],
        )(arrived[c], arrived[0], leaf_inverse, left_basis, right_basis, gram)

        level = local_levels
        solved = []
        for axis, bit, take in stages:
            group = [message]
            for mask in range(1, 1 << take):
                group.append(flipped(message, axis, mask << bit))
            scales = [1.0 / math.sqrt(leaf << (level + s)) for s in range(take)]
            left_over = levels - level - take
            shapes = [full((width, take * rank), BF16)]
            if left_over:
                shapes.append(full((band_rows(halves, left_over, rank), LANES), BF16))
            out = call(
                functools.partial(merge_kernel, take, rank, scales, width, levels - level),
                "merge",
                4,
                1 << 24,
                tuple(shapes),
                [vmem()] * len(group),
                (vmem(),) * len(shapes),
            )(*group)
            solved.append(out[0])
            message = out[-1]
            level += take

        back = call(
            functools.partial(back_kernel, local_levels, rank, len(solved)),
            "back",
            14,
            1 << 30,
            full((devices, half, LANES), BF16),
            [vmem()] * (3 + len(solved)),
            vmem(),
            [
                VMEM((rows + 8, LANES), F32),
                SMEM((parts * devices, LANES), I32),
                VMEM((devices * half, LANES), F32),
                pltpu.SemaphoreType.DMA,
            ],
        )(field, left_basis, spots, *solved)
        returned = exchange(back)
        results.append(
            call(
                final_kernel,
                "final",
                14,
                1 << 30,
                full((width, slots), BF16),
                [vmem(), vmem(), vmem()],
                vmem(),
                [
                    VMEM((devices * half, LANES), F32),
                    VMEM((slots, LANES), F32),
                    SMEM((blocks, LANES), I32),
                    pltpu.SemaphoreType.DMA,
                ],
            )(returned, row_of, part_of)
        )
    return results[0] if chunks == 1 else jnp.concatenate(results, axis=0)


def solution(mesh):
    in_specs = (
        P(None, ("leaf", "sub")),
        P(),
        P(("leaf", "sub")),
        P(("leaf", "sub"), None, None),
        P(None, None, ("leaf", "sub")),
        P(None, None, ("leaf", "sub")),
    )
    out_specs = P(None, ("leaf", "sub"))
    return jax.shard_map(body, mesh=mesh, in_specs=in_specs, out_specs=out_specs, check_vma=False)
```

profile of v0, /device:TPU:0, one launch (start us, length us, event | category | flops | bytes accessed | tf_op | source)
XLA Modules:
  0.0 98.9 jit_solution(18143056396134818034)
XLA Ops:
  0.0 0.0 copy-start.5
  0.0 1.1 %copy-done.5 = bf16[64,5120]{1,0:T(8,128)(2,1)S(1)} copy-done((bf16[64,5120]{1,0:T(8,128)(2,1)S(1)}, bf16[64,5120]{1,0:T(8,128)(2,1)}, u32[]{:S(2)}) %copy-start.5) | copy-done | bytes 655384
  1.1 0.0 copy-start.6
  1.1 0.7 copy-done.6
  1.8 0.0 copy-start.7
  1.8 0.7 copy-done.7
  2.5 0.0 copy-start
  2.5 7.7 %send.1 = (bf16[32,88,128]{2,1,0:T(8,128)(2,1)S(1)}, s32[40,128]{1,0:T(8,128)S(1)}, s32[40,128]{1,0:T(8,128)S(1)}) custom-call(s32[32]{0:T(128)S(1)} %copy-done.7, bf16[64,5120]{1,0:T(8,128)(2,1)S(1)} %copy-done.5, s32[40,128]{1,0:T(8,128)S(1)} %bitcast.1), custom_call_target="tpu_custom_call" | custom-call | flops 1073741824 | bytes 1048576 | tf_op jit(solution)/shard_map/send/pallas_call | solution.py:373
  10.1 0.0 copy-start.4
  10.2 0.9 copy-done.4
  11.0 7.3 %all-to-all-start = ((bf16[32,88,128]{2,1,0:T(8,128)(2,1)}), bf16[32,88,128]{2,1,0:T(8,128)(2,1)S(1)}, u32[]{:S(2)}, u32[]{:S(2)}) async-start(bf16[32,88,128]{2,1,0:T(8,128)(2,1)} %copy-done.4), calls=%async_computation | async-start | bytes 1441792 | tf_op jit(solution)/shard_map/all_to_all | solution.py:396
  18.4 0.0 copy-done
  18.4 0.0 copy-start.1
  18.4 1.7 %copy-done.1 = bf16[9,32,4096]{2,1,0:T(8,128)(2,1)S(1)} copy-done((bf16[9,32,4096]{2,1,0:T(8,128)(2,1)S(1)}, bf16[9,32,4096]{2,1,0:T(8,128)(2,1)}, u32[]{:S(2)}) %copy-start.1) | copy-done | bytes 2359320
  20.0 0.5 gram.1.gram_ref
  20.6 17.0 %all-to-all-done.arr_ref.pos_ref = bf16[32,88,128]{2,1,0:T(8,128)(2,1)S(1)} async-done(((bf16[32,88,128]{2,1,0:T(8,128)(2,1)}), bf16[32,88,128]{2,1,0:T(8,128)(2,1)S(1)}, u32[]{:S(2)}, u32[]{:S(2)}) %all-to-all-start) | async-done | bytes 720928 | tf_op jit(solution)/shard_map/all_to_all | solution.py:396
  37.5 0.0 copy-start.2
  37.5 1.7 %copy-done.2 = bf16[9,32,4096]{2,1,0:T(8,128)(2,1)S(1)} copy-done((bf16[9,32,4096]{2,1,0:T(8,128)(2,1)S(1)}, bf16[9,32,4096]{2,1,0:T(8,128)(2,1)}, u32[]{:S(2)}) %copy-start.2) | copy-done | bytes 2359320
  39.2 0.0 copy-start.3
  39.2 1.6 %copy-done.3 = bf16[16,256,256]{2,1,0:T(8,128)(2,1)S(1)} copy-done((bf16[16,256,256]{2,1,0:T(8,128)(2,1)S(1)}, bf16[16,256,256]{2,1,0:T(8,128)(2,1)}, u32[]{:S(2)}) %copy-start.3) | copy-done | bytes 2097176
  40.8 8.4 %tree.1 = (f32[64,4096]{1,0:T(8,128)S(1)}, bf16[160,128]{1,0:T(8,128)(2,1)S(1)}, s32[64,128]{1,0:T(8,128)S(1)}) custom-call(bf16[32,88,128]{2,1,0:T(8,128)(2,1)S(1)} %all-to-all-done.arr_ref.pos_ref, bf16[32,88,128]{2,1,0:T(8,128)(2,1)S(1)} %all-to-all-done.arr_ref.pos_ref, bf16[16,256,256]{2,1,0:T(8,128)(2,1)S(1)} %copy-done.3, ...), custom_call_target="tpu_custom_call" | custom-call | flops 1073741824 | bytes 1048576 | tf_op jit(solution)/shard_map/tree/pallas_call | solution.py:420
  49.3 1.4 %collective-permute-start.2 = (bf16[160,128]{1,0:T(8,128)(2,1)S(1)}, bf16[160,128]{1,0:T(8,128)(2,1)S(1)}, u32[]{:S(2)}, u32[]{:S(2)}) collective-permute-start(bf16[160,128]{1,0:T(8,128)(2,1)S(1)} %get-tuple-element.18.refs_0_), channel_id=1, source_target_pairs={{0,3},{1,2},{2,1},{3,0},{4,7},{5,6},{6,5},{7,4},{8,11},{9,10},{10,... | collective-permute-start | bytes 122888 | tf_op jit(solution)/shard_map/ppermute | solution.py:347
  50.7 0.4 collective-permute-start.1
  51.1 0.1 collective-permute-start
  51.2 1.7 %collective-permute-done.2.refs_3_ = bf16[160,128]{1,0:T(8,128)(2,1)S(1)} collective-permute-done((bf16[160,128]{1,0:T(8,128)(2,1)S(1)}, bf16[160,128]{1,0:T(8,128)(2,1)S(1)}, u32[]{:S(2)}, u32[]{:S(2)}) %collective-permute-start.2) | collective-permute-done | bytes 40992 | tf_op jit(solution)/shard_map/ppermute | solution.py:347
  52.9 1.8 %collective-permute-done.1.refs_2_ = bf16[160,128]{1,0:T(8,128)(2,1)S(1)} collective-permute-done((bf16[160,128]{1,0:T(8,128)(2,1)S(1)}, bf16[160,128]{1,0:T(8,128)(2,1)S(1)}, u32[]{:S(2)}, u32[]{:S(2)}) %collective-permute-start.1) | collective-permute-done | bytes 40992 | tf_op jit(solution)/shard_map/ppermute | solution.py:347
  54.7 0.0 collective-permute-done.refs_1_
  54.7 0.5 merge.3
  55.2 0.9 collective-permute-start.5
  56.1 1.8 %collective-permute-start.4 = (bf16[96,128]{1,0:T(8,128)(2,1)S(1)}, bf16[96,128]{1,0:T(8,128)(2,1)S(1)}, u32[]{:S(2)}, u32[]{:S(2)}) collective-permute-start(bf16[96,128]{1,0:T(8,128)(2,1)S(1)} %get-tuple-element.20.refs_0_), channel_id=1, source_target_pairs={{0,8},{4,12},{8,0},{12,4},{16,24},{20,28},{24,16},{28,20},{1,9},{5... | collective-permute-start | bytes 73736 | tf_op jit(solution)/shard_map/ppermute | solution.py:347
  57.9 0.8 collective-permute-start.3
  58.8 1.2 %collective-permute-done.5.refs_3_ = bf16[96,128]{1,0:T(8,128)(2,1)S(1)} collective-permute-done((bf16[96,128]{1,0:T(8,128)(2,1)S(1)}, bf16[96,128]{1,0:T(8,128)(2,1)S(1)}, u32[]{:S(2)}, u32[]{:S(2)}) %collective-permute-start.5) | collective-permute-done | bytes 24608 | tf_op jit(solution)/shard_map/ppermute | solution.py:347
  60.0 0.0 collective-permute-done.4.refs_2_
  60.0 1.8 %collective-permute-done.3.refs_1_ = bf16[96,128]{1,0:T(8,128)(2,1)S(1)} collective-permute-done((bf16[96,128]{1,0:T(8,128)(2,1)S(1)}, bf16[96,128]{1,0:T(8,128)(2,1)S(1)}, u32[]{:S(2)}, u32[]{:S(2)}) %collective-permute-start.3) | collective-permute-done | bytes 24608 | tf_op jit(solution)/shard_map/ppermute | solution.py:347
  61.8 0.5 merge.4
  62.3 0.0 collective-permute-start.6
  62.3 4.5 %collective-permute-done.6.refs_1_ = bf16[32,128]{1,0:T(8,128)(2,1)S(1)} collective-permute-done((bf16[32,128]{1,0:T(8,128)(2,1)S(1)}, bf16[32,128]{1,0:T(8,128)(2,1)S(1)}, u32[]{:S(2)}, u32[]{:S(2)}) %collective-permute-start.6) | collective-permute-done | bytes 8224 | tf_op jit(solution)/shard_map/ppermute | solution.py:347
  66.8 0.1 merge.5.refs_2_
  66.9 5.5 %back.1 = bf16[32,80,128]{2,1,0:T(8,128)(2,1)S(1)} custom-call(f32[64,4096]{1,0:T(8,128)S(1)} %get-tuple-element.16.field_ref, bf16[9,32,4096]{2,1,0:T(8,128)(2,1)S(1)} %copy-done, s32[64,128]{1,0:T(8,128)S(1)} %get-tuple-element.17.spot_ref, bf16[64,64]{1,0:T(8,128)(2,1)S(1)} %get-tuple-element.19.refs_0_, bf16[64,64]{1,0:T(8,128)(2,1)S(1)} %get-tuple-element.21.refs_1_, ...), custom_call_target="tpu_custom_call" | custom-call | flops 1073741824 | bytes 1048576 | tf_op jit(solution)/shard_map/back/pallas_call | solution.py:464
  72.4 20.2 %all_to_all.10.ret_ref = bf16[32,80,128]{2,1,0:T(8,128)(2,1)S(1)} all-to-all(bf16[32,80,128]{2,1,0:T(8,128)(2,1)S(1)} %back.1), channel_id=1, replica_groups=mesh['leaf'=8,'sub'=4] {'leaf','sub'}, dimensions={0} | all-to-all | bytes 1310720 | tf_op jit(solution)/shard_map/all_to_all | solution.py:396
  92.6 6.4 %final.1 = bf16[64,5120]{1,0:T(8,128)(2,1)} custom-call(bf16[32,80,128]{2,1,0:T(8,128)(2,1)S(1)} %all_to_all.10.ret_ref, s32[40,128]{1,0:T(8,128)S(1)} %get-tuple-element.23.row_ref, s32[40,128]{1,0:T(8,128)S(1)} %get-tuple-element.24.part_ref), custom_call_target="tpu_custom_call" | custom-call | flops 1073741824 | bytes 1048576 | tf_op jit(solution)/shard_map/final/pallas_call | solution.py:481
Async XLA Ops:
  0.0 1.1 %copy-start.5 = (bf16[64,5120]{1,0:T(8,128)(2,1)S(1)}, bf16[64,5120]{1,0:T(8,128)(2,1)}, u32[]{:S(2)}) copy-start(bf16[64,5120]{1,0:T(8,128)(2,1)} %vec_ref.1) | copy-start | bytes 1966084
  1.1 0.7 copy-start.6
  1.8 0.7 copy-start.7
  2.5 15.9 %copy-start = (bf16[9,32,4096]{2,1,0:T(8,128)(2,1)S(1)}, bf16[9,32,4096]{2,1,0:T(8,128)(2,1)}, u32[]{:S(2)}) copy-start(bf16[9,32,4096]{2,1,0:T(8,128)(2,1)} %left.5) | copy-start | bytes 7077892
  10.1 0.9 copy-start.4
  11.0 26.5 %all-to-all-start = ((bf16[32,88,128]{2,1,0:T(8,128)(2,1)}), bf16[32,88,128]{2,1,0:T(8,128)(2,1)S(1)}, u32[]{:S(2)}, u32[]{:S(2)}) async-start(bf16[32,88,128]{2,1,0:T(8,128)(2,1)} %copy-done.4), calls=%async_computation | async-start | bytes 1441792 | tf_op jit(solution)/shard_map/all_to_all | solution.py:396
  18.4 1.7 %copy-start.1 = (bf16[9,32,4096]{2,1,0:T(8,128)(2,1)S(1)}, bf16[9,32,4096]{2,1,0:T(8,128)(2,1)}, u32[]{:S(2)}) copy-start(bf16[9,32,4096]{2,1,0:T(8,128)(2,1)} %right.3) | copy-start | bytes 7077892
  37.5 1.7 %copy-start.2 = (bf16[9,32,4096]{2,1,0:T(8,128)(2,1)S(1)}, bf16[9,32,4096]{2,1,0:T(8,128)(2,1)}, u32[]{:S(2)}) copy-start(bf16[9,32,4096]{2,1,0:T(8,128)(2,1)} %right.3) | copy-start | bytes 7077892
  39.2 1.6 %copy-start.3 = (bf16[16,256,256]{2,1,0:T(8,128)(2,1)S(1)}, bf16[16,256,256]{2,1,0:T(8,128)(2,1)}, u32[]{:S(2)}) copy-start(bf16[16,256,256]{2,1,0:T(8,128)(2,1)} %inv.1) | copy-start | bytes 6291460
  49.3 3.7 %collective-permute-start.2 = (bf16[160,128]{1,0:T(8,128)(2,1)S(1)}, bf16[160,128]{1,0:T(8,128)(2,1)S(1)}, u32[]{:S(2)}, u32[]{:S(2)}) collective-permute-start(bf16[160,128]{1,0:T(8,128)(2,1)S(1)} %get-tuple-element.18.refs_0_), channel_id=1, source_target_pairs={{0,3},{1,2},{2,1},{3,0},{4,7},{5,6},{6,5},{7,4},{8,11},{9,10},{10,... | collective-permute-start | bytes 122888 | tf_op jit(solution)/shard_map/ppermute | solution.py:347
  50.7 4.0 %collective-permute-start.1 = (bf16[160,128]{1,0:T(8,128)(2,1)S(1)}, bf16[160,128]{1,0:T(8,128)(2,1)S(1)}, u32[]{:S(2)}, u32[]{:S(2)}) collective-permute-start(bf16[160,128]{1,0:T(8,128)(2,1)S(1)} %get-tuple-element.18.refs_0_), channel_id=1, source_target_pairs={{0,2},{1,3},{2,0},{3,1},{4,6},{5,7},{6,4},{7,5},{8,10},{9,11},{10,... | collective-permute-start | bytes 122888 | tf_op jit(solution)/shard_map/ppermute | solution.py:347
  51.1 3.6 %collective-permute-start = (bf16[160,128]{1,0:T(8,128)(2,1)S(1)}, bf16[160,128]{1,0:T(8,128)(2,1)S(1)}, u32[]{:S(2)}, u32[]{:S(2)}) collective-permute-start(bf16[160,128]{1,0:T(8,128)(2,1)S(1)} %get-tuple-element.18.refs_0_), channel_id=1, source_target_pairs={{0,1},{1,0},{2,3},{3,2},{4,5},{5,4},{6,7},{7,6},{8,9},{9,8},{10,11... | collective-permute-start | bytes 122888 | tf_op jit(solution)/shard_map/ppermute | solution.py:347
  55.2 4.8 %collective-permute-start.5 = (bf16[96,128]{1,0:T(8,128)(2,1)S(1)}, bf16[96,128]{1,0:T(8,128)(2,1)S(1)}, u32[]{:S(2)}, u32[]{:S(2)}) collective-permute-start(bf16[96,128]{1,0:T(8,128)(2,1)S(1)} %get-tuple-element.20.refs_0_), channel_id=1, source_target_pairs={{0,12},{4,8},{8,4},{12,0},{16,28},{20,24},{24,20},{28,16},{1,13},{... | collective-permute-start | bytes 73736 | tf_op jit(solution)/shard_map/ppermute | solution.py:347
  56.1 3.9 %collective-permute-start.4 = (bf16[96,128]{1,0:T(8,128)(2,1)S(1)}, bf16[96,128]{1,0:T(8,128)(2,1)S(1)}, u32[]{:S(2)}, u32[]{:S(2)}) collective-permute-start(bf16[96,128]{1,0:T(8,128)(2,1)S(1)} %get-tuple-element.20.refs_0_), channel_id=1, source_target_pairs={{0,8},{4,12},{8,0},{12,4},{16,24},{20,28},{24,16},{28,20},{1,9},{5... | collective-permute-start | bytes 73736 | tf_op jit(solution)/shard_map/ppermute | solution.py:347
  57.9 3.8 %collective-permute-start.3 = (bf16[96,128]{1,0:T(8,128)(2,1)S(1)}, bf16[96,128]{1,0:T(8,128)(2,1)S(1)}, u32[]{:S(2)}, u32[]{:S(2)}) collective-permute-start(bf16[96,128]{1,0:T(8,128)(2,1)S(1)} %get-tuple-element.20.refs_0_), channel_id=1, source_target_pairs={{0,4},{4,0},{8,12},{12,8},{16,20},{20,16},{24,28},{28,24},{1,5},{5... | collective-permute-start | bytes 73736 | tf_op jit(solution)/shard_map/ppermute | solution.py:347
  62.3 4.6 %collective-permute-start.6 = (bf16[32,128]{1,0:T(8,128)(2,1)S(1)}, bf16[32,128]{1,0:T(8,128)(2,1)S(1)}, u32[]{:S(2)}, u32[]{:S(2)}) collective-permute-start(bf16[32,128]{1,0:T(8,128)(2,1)S(1)} %get-tuple-element.22.refs_0_), channel_id=1, source_target_pairs={{0,16},{4,20},{8,24},{12,28},{16,0},{20,4},{24,8},{28,12},{1,17},{... | collective-permute-start | bytes 24584 | tf_op jit(solution)/shard_map/ppermute | solution.py:347
where the time goes:
time: 99.3 us; the launch traced here: 98.9 us
  Pallas kernels  29.6 us (30%)
  waiting for transfers between devices  28 us (28%)
  blocking collectives  20.2 us (20%)
  starting transfers between devices  12.8 us (13%)
  local copies, waits for them, and re-layouts  8.26 us (8%)
    all_to_all x1, blocking collectives, exchange(): return lax.all_to_all(x, axes, split_axis=0, concat_axis=0, tiled=True)  20.2 us
    all_to_all x1, waiting for transfers between devices, exchange(): return lax.all_to_all(x, axes, split_axis=0, concat_axis=0, tiled=True)  17 us
    ppermute x7, waiting for transfers between devices, flipped(): return lax.ppermute(block, axis, [(i, i ^ mask) for i in range(count)])  11 us
    pallas_call x1, Pallas kernels, body(): call(functools.partial(tree_kernel, local_levels, leaf, rank), 'tree', 20...  8.45 us
    unnamed x16, local copies, waits for them, and re-layouts  8.26 us
    pallas_call x1, Pallas kernels, body(): call(functools.partial(send_kernel, rows, vecs, chunks, half, n_sub), 'se...  7.67 us
    all_to_all x1, starting transfers between devices, exchange(): return lax.all_to_all(x, axes, split_axis=0, concat_axis=0, tiled=True)  7.33 us
    pallas_call x1, Pallas kernels, body(): call(final_kernel, 'final', 14, 1 << 30, full((width, slots), BF16), [vme...  6.36 us
  transfers between devices with their start and end apart: 8, of which 6 were waited for; matrix products, arithmetic and copies ran while one was open for 0% of the time, Pallas kernels for 1%

commit v1 on v0

v1 whole, which is shorter than its diff:
```python
import functools
import math

import jax
import jax.numpy as jnp
from jax import lax
from jax.experimental import pallas as pl
from jax.experimental.pallas import tpu as pltpu
from jax.sharding import PartitionSpec as P

F32 = jnp.float32
BF16 = jnp.bfloat16
I32 = jnp.int32
LANES = 128
DIGIT = 64
NT = (((1,), (1,)), ((), ()))
VMEM = pltpu.VMEM
SMEM = pltpu.SMEM
FINAL_UNROLL = 40
PLACE_UNROLL = 32
PICK_UNROLL = 32
SEND_UNROLL = 1


def dot(a, b):
    return jnp.dot(a, b, preferred_element_type=F32)


def dot_nt(a, b):
    return lax.dot_general(a, b, NT, preferred_element_type=F32)


def iota(shape, dim):
    return lax.broadcasted_iota(I32, shape, dim)


def rows_at(start, size):
    return pl.ds(pl.multiple_of(start, 8), size)


def send_kernel(
    rows, vecs, half, n_sub, first, counts_hbm, vec_hbm, slot_hbm, left_hbm, right_hbm,
    out_ref, row_ref, part_ref, gram_ref,
    counts, vec, slots, left, right, xt, staged, flat, places, owners, codes, pos, posf, sems,
):
    devices = out_ref.shape[0]
    parts = LANES // vecs
    blocks = slots.shape[0]
    levels = left_hbm.shape[0]
    cross = levels - first
    loads = [
        pltpu.make_async_copy(counts_hbm, counts, sems.at[0]),
        pltpu.make_async_copy(slot_hbm, slots, sems.at[1]),
        pltpu.make_async_copy(vec_hbm, vec, sems.at[2]),
        pltpu.make_async_copy(left_hbm.at[pl.ds(first, cross)], left, sems.at[3]),
        pltpu.make_async_copy(right_hbm.at[pl.ds(first, cross)], right, sems.at[4]),
    ]
    for load in loads:
        load.start()
    trash = devices * parts * half
    shift = rows.bit_length() - 1
    owner_id = iota((devices, LANES), 0)
    before = (iota((LANES, LANES), 0) < iota((LANES, LANES), 1)).astype(BF16)
    ones = jnp.ones((LANES, LANES), BF16)
    carry = jnp.zeros((devices, LANES), F32)
    loads[0].wait()
    loads[1].wait()
    count = counts[lax.axis_index("leaf") * n_sub + lax.axis_index("sub")]
    for b in range(blocks):
        slot = slots[b : b + 1, :]
        lane = iota((1, LANES), 1) + b * LANES
        live = (lane < count) & (slot >= 0)
        owner = jnp.where(live, slot >> shift, -1)
        hot = owner_id == owner
        hot_b = jnp.where(hot, 1.0, 0.0).astype(BF16)
        ranks = dot(hot_b, before) + carry
        carry = carry + dot(hot_b, ones)
        rank = jnp.sum(jnp.where(hot, ranks, 0.0), axis=0, keepdims=True).astype(I32)
        flat[b : b + 1, :] = jnp.where(live, owner * (parts * half) + rank, trash)
        part = jnp.zeros((1, LANES), I32)
        for q in range(1, parts):
            part = part + jnp.where(rank >= q * half, 1, 0)
        inner = rank - part * half
        row_ref[b : b + 1, :] = jnp.where(live, owner * half + inner, 0)
        part_ref[b : b + 1, :] = jnp.where(live, part, parts)
        owners[b : b + 1, :] = owner
        codes[b : b + 1, :] = part * LANES + inner
    copy = pltpu.make_async_copy(flat, places, sems.at[5])
    copy.start()
    for load in loads[2:]:
        load.wait()
    pos[...] = jnp.zeros(pos.shape, F32)
    gram_ref[...] = jnp.zeros(gram_ref.shape, F32)
    code_id = iota((parts * LANES, LANES), 0)
    tile = 256
    tiles = rows // tile

    def turn(b, _):
        at = pl.multiple_of(b * LANES, LANES)
        x = vec[:, pl.ds(at, LANES)].astype(F32)
        xt[pl.ds(at, LANES), :] = jnp.concatenate([x] * parts, axis=0).T
        return 0

    lax.fori_loop(0, blocks, turn, 0, unroll=8)
    copy.wait()

    def move(i, _):
        digits, spread = [], []
        for s in range(2):
            b = 2 * i + s
            hot = owner_id == owners[pl.ds(b, 1), :]
            local = slots[pl.ds(b, 1), :] & (rows - 1)
            high = ((local >> 6) + 1).astype(F32)
            low = (local & (DIGIT - 1)).astype(F32)
            digits.append(
                jnp.concatenate([jnp.where(hot, high, 0.0), jnp.where(hot, low, 0.0)], axis=0)
            )
            spread.append(jnp.where(code_id == codes[pl.ds(b, 1), :], 1.0, 0.0))
            for u in range(LANES):
                staged[pl.ds(places[b, u], 1), :] = xt[pl.ds(b * LANES + u, 1), :]
        pos[...] = pos[...] + dot_nt(
            jnp.concatenate(digits, axis=1).astype(BF16),
            jnp.concatenate(spread, axis=1).astype(BF16),
        )
        at = pl.ds(pl.multiple_of(jnp.minimum(i, tiles - 1) * tile, tile), tile)
        keep = jnp.where(i < tiles, 1.0, 0.0)
        lhs = jnp.concatenate([left[k, :, at] for k in range(cross)], axis=0)
        rhs = jnp.concatenate([right[k, :, at] for k in range(cross)], axis=0)
        gram_ref[...] = gram_ref[...] + dot_nt(lhs, rhs) * keep
        return 0

    lax.fori_loop(0, blocks // 2, move, 0, unroll=SEND_UNROLL)
    for d in range(devices):
        for q in range(parts):
            at = slice(q * LANES, (q + 1) * LANES)
            posf[8 * d + q : 8 * d + q + 1, :] = pos[d : d + 1, at]
            posf[8 * d + parts + q : 8 * d + parts + q + 1, :] = pos[devices + d : devices + d + 1, at]
    group = iota((half, LANES), 1) // vecs

    def pack(d, _):
        packed = staged[rows_at(d * parts * half, half), :]
        for q in range(1, parts):
            packed = jnp.where(group == q, staged[rows_at((d * parts + q) * half, half), :], packed)
        out_ref[d, pl.ds(0, half), :] = packed.astype(BF16)
        out_ref[d, pl.ds(half, 8), :] = posf[rows_at(d * 8, 8), :].astype(BF16)
        return 0

    lax.fori_loop(0, devices, pack, 0)


def band_tiles(halves, levels):
    tiles = [("b", h, k) for k in range(levels) for h in range(halves)]
    return tiles + [("g", j, k) for j in range(levels) for k in range(j + 1, levels)]


def band_rows(halves, levels, rank):
    return (len(band_tiles(halves, levels)) + 3) // 4 * rank


def pack_bands(ref, b, gram, rank, halves, levels):
    tiles = band_tiles(halves, levels)
    blank = jnp.zeros((rank, rank), F32)
    for r in range(0, len(tiles), 4):
        band = []
        for kind, x, k in tiles[r : r + 4]:
            at = slice(k * rank, (k + 1) * rank)
            band.append(b[x * rank : (x + 1) * rank, at] if kind == "b" else gram[x][:, at])
        band += [blank] * (4 - len(band))
        ref[r // 4 * rank : (r // 4 + 1) * rank, :] = jnp.concatenate(band, axis=1).astype(BF16)


def unpack_bands(value, rank, halves, levels):
    tiles = band_tiles(halves, levels)
    found = {}
    for t, key in enumerate(tiles):
        found[key] = value[t // 4 * rank : (t // 4 + 1) * rank, t % 4 * rank : (t % 4 + 1) * rank]
    b = jnp.concatenate(
        [
            jnp.concatenate([found["b", h, k] for k in range(levels)], axis=1)
            for h in range(halves)
        ],
        axis=0,
    )
    blank = jnp.zeros((rank, rank), F32)
    gram = [
        jnp.concatenate([found["g", j, k] if k > j else blank for k in range(levels)], axis=1)
        for j in range(levels)
    ]
    return b, gram


def tree_kernel(
    local_levels, leaf, rank, arr_ref, inv_hbm, left_hbm, right_hbm, gram_ref,
    field_ref, message_ref, spot_ref, arr, tree, inv, left, right, spots, sems,
):
    devices = arr_ref.shape[0]
    vecs, rows = field_ref.shape
    parts = LANES // vecs
    half = arr.shape[0] // devices
    leaves = rows // leaf
    levels = right_hbm.shape[0]
    loads = [
        pltpu.make_async_copy(inv_hbm, inv, sems.at[0]),
        pltpu.make_async_copy(right_hbm, right, sems.at[1]),
        pltpu.make_async_copy(left_hbm.at[pl.ds(0, local_levels)], left, sems.at[2]),
    ]
    for load in loads:
        load.start()
    for d in range(devices):
        pos = arr_ref[d, half : half + 8, :].astype(F32)
        high = pos[0:parts, :]
        low = pos[parts : 2 * parts, :]
        spot = jnp.where(high > 0.5, (high - 1.0) * DIGIT + low, float(rows)).astype(I32)
        spot_ref[parts * d : parts * (d + 1), :] = spot
    copy = pltpu.make_async_copy(spot_ref, spots, sems.at[3])
    copy.start()

    def widen(d, _):
        arr[rows_at(d * half, half), :] = arr_ref[d, pl.ds(0, half), :].astype(F32)
        return 0

    lax.fori_loop(0, devices, widen, 0)

    def clear(i, _):
        tree[rows_at(i * 128, 128), :] = jnp.zeros((128, LANES), F32)
        return 0

    lax.fori_loop(0, rows // 128, clear, 0)
    copy.wait()

    def place(d, _):
        for u in range(half):
            row = arr[pl.ds(d * half + u, 1), :]
            for q in range(parts):
                at = pl.ds(spots[parts * d + q, u], 1)
                tree[at, pl.ds(q * vecs, vecs)] = row[:, q * vecs : (q + 1) * vecs]
        return 0

    lax.fori_loop(0, devices, place, 0, unroll=PLACE_UNROLL)
    for load in loads:
        load.wait()
    for l in range(leaves):
        block = tree[l * leaf : (l + 1) * leaf, :].astype(BF16)
        turned = dot(inv[l], block).T
        total = turned[:vecs]
        for q in range(1, parts):
            total = total + turned[q * vecs : (q + 1) * vecs]
        field_ref[:, l * leaf : (l + 1) * leaf] = total
    for k in range(local_levels):
        size = leaf << k
        scale = 1.0 / math.sqrt(size)
        coeff = []
        for n in range(rows // size):
            at = slice(n * size, (n + 1) * size)
            part = dot_nt(field_ref[:, at].astype(BF16), right[k, :, at])
            coeff.append((part * scale).astype(BF16))
        for n in range(rows // size):
            at = slice(n * size, (n + 1) * size)
            field_ref[:, at] = field_ref[:, at] - dot(coeff[n ^ 1], left[k, :, at])
    rounded = field_ref[...].astype(BF16)
    cross = levels - local_levels
    b = jnp.concatenate([dot_nt(rounded, right[k]) for k in range(local_levels, levels)], axis=1)
    gram = [gram_ref[j * rank : (j + 1) * rank, :] for j in range(cross)]
    pack_bands(message_ref, b, gram, rank, vecs // rank, cross)


def merge_kernel(bits, rank, scales, vecs, levels, *refs):
    group = 1 << bits
    p_ref = refs[group]
    halves = vecs // rank
    found = [unpack_bands(r[...].astype(F32), rank, halves, levels) for r in refs[:group]]
    b = [f[0] for f in found]
    gram = [f[1] for f in found]
    for step in range(bits):
        at = slice(step * rank, (step + 1) * rank)
        p = [(b[x ^ 1][:, at] * scales[step]).astype(BF16) for x in range(len(b))]
        p_ref[:, at] = p[0]
        if step + 1 < levels:
            b = [b[x] - dot(p[x], gram[x][step].astype(BF16)) for x in range(len(b))]
            b = [b[x] + b[x + 1] for x in range(0, len(b), 2)]
            gram = [
                [u + v for u, v in zip(gram[x], gram[x + 1])] for x in range(0, len(gram), 2)
            ]
    if levels > bits:
        keep = slice(bits * rank, levels * rank)
        rest = [g[:, keep] for g in gram[0][bits:]]
        pack_bands(refs[group + 1], b[0][:, keep], rest, rank, halves, levels - bits)


def back_kernel(first, rank, n_solved, field_ref, left, spot_ref, *refs):
    solved = refs[:n_solved]
    out_ref, done, spots, packed, sem = refs[n_solved:]
    devices, half, _ = out_ref.shape
    vecs, rows = field_ref.shape
    parts = LANES // vecs
    levels = left.shape[0]
    copy = pltpu.make_async_copy(spot_ref, spots, sem)
    copy.start()
    p = jnp.concatenate([r[...] for r in solved], axis=1)
    wide = 512
    for c in range(rows // wide):
        at = slice(c * wide, (c + 1) * wide)
        basis = jnp.concatenate([left[k, :, at] for k in range(first, levels)], axis=0)
        field = field_ref[:, at] - dot(p, basis)
        for q in range(wide // LANES):
            x = field[:, q * LANES : (q + 1) * LANES]
            low = c * wide + q * LANES
            done[low : low + LANES, :] = jnp.concatenate([x] * parts, axis=0).T
    copy.wait()
    group = iota((1, LANES), 1) // vecs

    def pick(d, _):
        for u in range(half):
            row = done[pl.ds(spots[parts * d, u], 1), :]
            for q in range(1, parts):
                row = jnp.where(group == q, done[pl.ds(spots[parts * d + q, u], 1), :], row)
            packed[pl.ds(d * half + u, 1), :] = row
        return 0

    lax.fori_loop(0, devices, pick, 0, unroll=PICK_UNROLL)

    def narrow(d, _):
        out_ref[d, :, :] = packed[rows_at(d * half, half), :].astype(BF16)
        return 0

    lax.fori_loop(0, devices, narrow, 0)


def final_kernel(ret_ref, row_ref, part_ref, out_ref, ret, picked, places, sem):
    devices, half, _ = ret_ref.shape
    vecs = out_ref.shape[0]
    parts = LANES // vecs
    blocks = row_ref.shape[0]
    copy = pltpu.make_async_copy(row_ref, places, sem)
    copy.start()

    def widen(d, _):
        ret[rows_at(d * half, half), :] = ret_ref[d, :, :].astype(F32)
        return 0

    lax.fori_loop(0, devices, widen, 0)
    copy.wait()

    def move(b, _):
        for u in range(LANES):
            picked[pl.ds(b * LANES + u, 1), :] = ret[pl.ds(places[b, u], 1), :]
        return 0

    lax.fori_loop(0, blocks, move, 0, unroll=FINAL_UNROLL)
    for b in range(blocks):
        x = picked[b * LANES : (b + 1) * LANES, :].T
        part = part_ref[b : b + 1, :]
        value = jnp.zeros((vecs, LANES), F32)
        for q in range(parts):
            value = jnp.where(part == q, x[q * vecs : (q + 1) * vecs], value)
        out_ref[:, b * LANES : (b + 1) * LANES] = value.astype(BF16)


def full(shape, dtype):
    return jax.ShapeDtypeStruct(shape, dtype)


def vmem():
    return pl.BlockSpec(memory_space=VMEM)


def hbm():
    return pl.BlockSpec(memory_space=pltpu.HBM)


def call(kernel, name, mib, flops, out_shape, in_specs, out_specs, scratch_shapes=()):
    return pl.pallas_call(
        kernel,
        out_shape=out_shape,
        in_specs=in_specs,
        out_specs=out_specs,
        scratch_shapes=scratch_shapes,
        compiler_params=pltpu.CompilerParams(vmem_limit_bytes=mib << 20),
        cost_estimate=pl.CostEstimate(flops=flops, bytes_accessed=1 << 20, transcendentals=0),
        name=name,
    )


def stay(x):
    return pltpu.with_memory_space_constraint(x, pltpu.HBM)


def flipped(block, axes, mask):
    count = lax.axis_size(axes)
    return lax.ppermute(block, axes, [(i, i ^ mask) for i in range(count)])


def body(vectors, row_counts, tree_slot, leaf_inverse, left_basis, right_basis):
    vecs, slots = vectors.shape
    leaves, leaf = leaf_inverse.shape[0], leaf_inverse.shape[1]
    rows = leaves * leaf
    levels, rank = left_basis.shape[0], left_basis.shape[1]
    n_leaf = lax.axis_size("leaf")
    n_sub = lax.axis_size("sub")
    devices = n_leaf * n_sub
    cross = devices.bit_length() - 1
    local_levels = levels - cross
    cap = (slots + devices - 1) // devices
    blocks = slots // LANES
    axes = ("leaf", "sub")
    parts = LANES // vecs
    half = ((cap + parts - 1) // parts + 7) // 8 * 8
    if vecs * 2 != LANES or half > LANES or slots % (2 * LANES) or rows & (rows - 1):
        raise ValueError("unsupported sizes")
    if rows // 256 > blocks // 2 or devices != 1 << cross:
        raise ValueError("unsupported sizes")

    outgoing, row_of, part_of, gram = call(
        functools.partial(send_kernel, rows, vecs, half, n_sub, local_levels),
        "send",
        20,
        1 << 30,
        (
            full((devices, half + 8, LANES), BF16),
            full((blocks, LANES), I32),
            full((blocks, LANES), I32),
            full((cross * rank, cross * rank), F32),
        ),
        [hbm()] * 5,
        (vmem(),) * 4,
        [
            SMEM((devices,), I32),
            VMEM((vecs, slots), BF16),
            VMEM((blocks, LANES), I32),
            VMEM((cross, rank, rows), BF16),
            VMEM((cross, rank, rows), BF16),
            VMEM((slots, LANES), F32),
            VMEM((devices * parts * half + 8, LANES), F32),
            VMEM((blocks, LANES), I32),
            SMEM((blocks, LANES), I32),
            VMEM((blocks, LANES), I32),
            VMEM((blocks, LANES), I32),
            VMEM((2 * devices, parts * LANES), F32),
            VMEM((8 * devices, LANES), F32),
            pltpu.SemaphoreType.DMA((6,)),
        ],
    )(*map(stay, (row_counts, vectors, tree_slot.reshape(blocks, LANES), left_basis, right_basis)))

    def exchange(x):
        return lax.all_to_all(x, axes, split_axis=0, concat_axis=0, tiled=True)

    arrived = exchange(outgoing)
    halves = vecs // rank
    field, message, spots = call(
        functools.partial(tree_kernel, local_levels, leaf, rank),
        "tree",
        20,
        1 << 30,
        (
            full((vecs, rows), F32),
            full((band_rows(halves, cross, rank), LANES), BF16),
            full((parts * devices, LANES), I32),
        ),
        [vmem(), hbm(), hbm(), hbm(), vmem()],
        (vmem(), vmem(), vmem()),
        [
            VMEM((devices * half, LANES), F32),
            VMEM((rows + 8, LANES), F32),
            VMEM((leaves, leaf, leaf), BF16),
            VMEM((local_levels, rank, rows), BF16),
            VMEM((levels, rank, rows), BF16),
            SMEM((parts * devices, LANES), I32),
            pltpu.SemaphoreType.DMA((4,)),
        ],
    )(arrived, stay(leaf_inverse), stay(left_basis), stay(right_basis), gram)

    solved = []
    bit = 0
    while bit < cross:
        take = 1 if (cross - bit) % 2 else 2
        level = local_levels + bit
        group = [message] + [flipped(message, axes, m << bit) for m in range(1, 1 << take)]
        scales = [1.0 / math.sqrt(leaf << (level + s)) for s in range(take)]
        left_over = cross - bit - take
        shapes = [full((vecs, take * rank), BF16)]
        if left_over:
            shapes.append(full((band_rows(halves, left_over, rank), LANES), BF16))
        out = call(
            functools.partial(merge_kernel, take, rank, scales, vecs, cross - bit),
            "merge",
            4,
            1 << 24,
            tuple(shapes),
            [vmem()] * len(group),
            (vmem(),) * len(shapes),
        )(*group)
        solved.append(out[0])
        message = out[-1]
        bit += take

    back = call(
        functools.partial(back_kernel, local_levels, rank, len(solved)),
        "back",
        14,
        1 << 30,
        full((devices, half, LANES), BF16),
        [vmem()] * (3 + len(solved)),
        vmem(),
        [
            VMEM((rows + 8, LANES), F32),
            SMEM((parts * devices, LANES), I32),
            VMEM((devices * half, LANES), F32),
            pltpu.SemaphoreType.DMA,
        ],
    )(field, left_basis, spots, *solved)
    returned = exchange(back)
    return call(
        final_kernel,
        "final",
        14,
        1 << 30,
        full((vecs, slots), BF16),
        [vmem(), vmem(), vmem()],
        vmem(),
        [
            VMEM((devices * half, LANES), F32),
            VMEM((slots, LANES), F32),
            SMEM((blocks, LANES), I32),
            pltpu.SemaphoreType.DMA,
        ],
    )(returned, row_of, part_of)


def solution(mesh):
    in_specs = (
        P(None, ("leaf", "sub")),
        P(),
        P(("leaf", "sub")),
        P(("leaf", "sub"), None, None),
        P(None, None, ("leaf", "sub")),
        P(None, None, ("leaf", "sub")),
    )
    out_specs = P(None, ("leaf", "sub"))
    return jax.shard_map(body, mesh=mesh, in_specs=in_specs, out_specs=out_specs, check_vma=False)
```

time: 99.3 us -> 87.5 us (0.88)
  blocking collectives: 20.2 us -> 47.6 us
  waiting for transfers between devices: 28 us -> 6.35 us
  local copies, waits for them, and re-layouts: 8.26 us -> 0.01 us
  starting transfers between devices: 12.8 us -> 8.15 us
  Pallas kernels: 29.6 us -> 25 us
    all_to_all x1 -> x2, blocking collectives: 20.2 us -> 47.6 us  [exchange(): return lax.all_to_all(x, axes, split_axis=0, concat_axis=0, tiled=True)]
    all_to_all x1 -> x0, waiting for transfers between devices: 17 us -> none  [exchange(): return lax.all_to_all(x, axes, split_axis=0, concat_axis=0, tiled=True)]
    unnamed x16 -> x2, local copies, waits for them, and re-layouts: 8.26 us -> 0.01 us
    all_to_all x1 -> x0, starting transfers between devices: 7.33 us -> none  [exchange(): return lax.all_to_all(x, axes, split_axis=0, concat_axis=0, tiled=True)]
    ppermute x7, waiting for transfers between devices: 11 us -> 6.35 us  [flipped(): return lax.ppermute(block, axes, [(i, i ^ mask) for i in range(count)])]
    ppermute x7, starting transfers between devices: 5.5 us -> 8.15 us  [flipped(): return lax.ppermute(block, axes, [(i, i ^ mask) for i in range(count)])]
    pallas_call x6 -> x5, Pallas kernels: 15.6 us -> 14 us  [the longest x1 7.58 us: body(): call(functools.partial(send_kernel, rows, vecs, half, n_sub, local_levels...]
    pallas_call x1, Pallas kernels: 5.5 us -> 3.97 us  [body(): call(functools.partial(back_kernel, local_levels, rank, len(solved)), 'ba...]
  transfers between devices with their start and end apart: 8 -> 7, of which waited for: 6 -> 7; matrix products, arithmetic and copies ran while one was open for 0% -> 0% of each run, Pallas kernels for 1% -> 0%
where the time goes in v1:
time: 87.5 us; the launch traced here: 87.3 us
  blocking collectives  47.6 us (54%)
  Pallas kernels  25 us (29%)
  starting transfers between devices  8.15 us (9%)
  waiting for transfers between devices  6.35 us (7%)
    all_to_all x2, blocking collectives, exchange(): return lax.all_to_all(x, axes, split_axis=0, concat_axis=0, tiled=True)  47.6 us
    ppermute x7, starting transfers between devices, flipped(): return lax.ppermute(block, axes, [(i, i ^ mask) for i in range(count)])  8.15 us
    pallas_call x1, Pallas kernels, body(): call(functools.partial(send_kernel, rows, vecs, half, n_sub, local_levels...  7.58 us
    pallas_call x1, Pallas kernels, body(): call(functools.partial(tree_kernel, local_levels, leaf, rank), 'tree', 20...  6.96 us
    ppermute x7, waiting for transfers between devices, flipped(): return lax.ppermute(block, axes, [(i, i ^ mask) for i in range(count)])  6.35 us
    pallas_call x1, Pallas kernels, body(): call(final_kernel, 'final', 14, 1 << 30, full((vecs, slots), BF16), [vmem...  5.46 us
    pallas_call x1, Pallas kernels, body(): call(functools.partial(back_kernel, local_levels, rank, len(solved)), 'ba...  3.97 us
  transfers between devices with their start and end apart: 7, of which 7 were waited for; matrix products, arithmetic and copies ran while one was open for 0% of the time, Pallas kernels for 0%

profile of v1, /device:TPU:0, one launch (start us, length us, event | category | flops | bytes accessed | tf_op | source)
XLA Modules:
  0.0 87.3 jit_solution(8988859612563870742)
XLA Ops:
  0.0 7.6 %send.1 = (bf16[32,88,128]{2,1,0:T(8,128)(2,1)S(1)}, s32[40,128]{1,0:T(8,128)S(1)}, s32[40,128]{1,0:T(8,128)S(1)}, f32[160,160]{1,0:T(8,128)S(1)}) custom-call(s32[32]{0:T(128)} %counts_hbm.1, bf16[64,5120]{1,0:T(8,128)(2,1)} %vec_hbm.1, s32[40,128]{1,0:T(8,128)} %bitcast.1, bf16[9,32,4096]{2,1,0:T(8,128)(2,1)} %left.1, bf16[9,32,4096]{2,1,0:T(8,128)(2,1)} %right_hbm.3), custom_call_target="tpu_custom_call" | custom-call | flops 1073741824 | bytes 1048576 | tf_op jit(solution)/shard_map/send/pallas_call | solution.py:413
  7.6 26.3 %all_to_all.10.arr_ref = bf16[32,88,128]{2,1,0:T(8,128)(2,1)S(1)} all-to-all(bf16[32,88,128]{2,1,0:T(8,128)(2,1)S(1)} %get-tuple-element.16), channel_id=1, replica_groups=mesh['leaf'=8,'sub'=4] {'leaf','sub'}, dimensions={0} | all-to-all | bytes 1441792 | tf_op jit(solution)/shard_map/all_to_all | solution.py:445
  33.9 0.0 copy-start
  33.9 7.0 %tree.1 = (f32[64,4096]{1,0:T(8,128)S(1)}, bf16[160,128]{1,0:T(8,128)(2,1)S(1)}, s32[64,128]{1,0:T(8,128)S(1)}) custom-call(bf16[32,88,128]{2,1,0:T(8,128)(2,1)S(1)} %all_to_all.10.arr_ref, bf16[16,256,256]{2,1,0:T(8,128)(2,1)} %inv_hbm.1, bf16[9,32,4096]{2,1,0:T(8,128)(2,1)} %left.1, bf16[9,32,4096]{2,1,0:T(8,128)(2,1)} %right_hbm.3, ...), custom_call_target="tpu_custom_call" | custom-call | flops 1073741824 | bytes 1048576 | tf_op jit(solution)/shard_map/tree/pallas_call | solution.py:449
  40.9 0.2 collective-permute-start
  41.1 1.1 %collective-permute-done.refs_1_ = bf16[160,128]{1,0:T(8,128)(2,1)S(1)} collective-permute-done((bf16[160,128]{1,0:T(8,128)(2,1)S(1)}, bf16[160,128]{1,0:T(8,128)(2,1)S(1)}, u32[]{:S(2)}, u32[]{:S(2)}) %collective-permute-start) | collective-permute-done | bytes 40992 | tf_op jit(solution)/shard_map/ppermute | solution.py:390
  42.2 0.3 merge.3
  42.5 2.5 %collective-permute-start.3 = (bf16[128,128]{1,0:T(8,128)(2,1)S(1)}, bf16[128,128]{1,0:T(8,128)(2,1)S(1)}, u32[]{:S(2)}, u32[]{:S(2)}) collective-permute-start(bf16[128,128]{1,0:T(8,128)(2,1)S(1)} %get-tuple-element.22.refs_0_), channel_id=1, source_target_pairs={{0,6},{1,7},{2,4},{3,5},{4,2},{5,3},{6,0},{7,1},{8,14},{9,15},{10,... | collective-permute-start | bytes 98312 | tf_op jit(solution)/shard_map/ppermute | solution.py:390
  44.9 0.5 collective-permute-start.2
  45.5 0.5 collective-permute-start.1
  46.0 1.3 %collective-permute-done.3.refs_3_ = bf16[128,128]{1,0:T(8,128)(2,1)S(1)} collective-permute-done((bf16[128,128]{1,0:T(8,128)(2,1)S(1)}, bf16[128,128]{1,0:T(8,128)(2,1)S(1)}, u32[]{:S(2)}, u32[]{:S(2)}) %collective-permute-start.3) | collective-permute-done | bytes 32800 | tf_op jit(solution)/shard_map/ppermute | solution.py:390
  47.4 1.5 %collective-permute-done.2.refs_2_ = bf16[128,128]{1,0:T(8,128)(2,1)S(1)} collective-permute-done((bf16[128,128]{1,0:T(8,128)(2,1)S(1)}, bf16[128,128]{1,0:T(8,128)(2,1)S(1)}, u32[]{:S(2)}, u32[]{:S(2)}) %collective-permute-start.2) | collective-permute-done | bytes 32800 | tf_op jit(solution)/shard_map/ppermute | solution.py:390
  48.9 0.5 collective-permute-done.1.refs_1_
  49.4 0.5 merge.4
  49.9 1.5 %collective-permute-start.6 = (bf16[64,128]{1,0:T(8,128)(2,1)S(1)}, bf16[64,128]{1,0:T(8,128)(2,1)S(1)}, u32[]{:S(2)}, u32[]{:S(2)}) collective-permute-start(bf16[64,128]{1,0:T(8,128)(2,1)S(1)} %get-tuple-element.24.refs_0_), channel_id=1, source_target_pairs={{0,24},{1,25},{2,26},{3,27},{4,28},{5,29},{6,30},{7,31},{8,16},{9,... | collective-permute-start | bytes 49160 | tf_op jit(solution)/shard_map/ppermute | solution.py:390
  51.4 0.7 collective-permute-start.5
  52.1 2.2 %collective-permute-start.4 = (bf16[64,128]{1,0:T(8,128)(2,1)S(1)}, bf16[64,128]{1,0:T(8,128)(2,1)S(1)}, u32[]{:S(2)}, u32[]{:S(2)}) collective-permute-start(bf16[64,128]{1,0:T(8,128)(2,1)S(1)} %get-tuple-element.24.refs_0_), channel_id=1, source_target_pairs={{0,8},{1,9},{2,10},{3,11},{4,12},{5,13},{6,14},{7,15},{8,0},{9,1},... | collective-permute-start | bytes 49160 | tf_op jit(solution)/shard_map/ppermute | solution.py:390
  54.3 1.1 %collective-permute-done.6.refs_3_ = bf16[64,128]{1,0:T(8,128)(2,1)S(1)} collective-permute-done((bf16[64,128]{1,0:T(8,128)(2,1)S(1)}, bf16[64,128]{1,0:T(8,128)(2,1)S(1)}, u32[]{:S(2)}, u32[]{:S(2)}) %collective-permute-start.6) | collective-permute-done | bytes 16416 | tf_op jit(solution)/shard_map/ppermute | solution.py:390
  55.5 0.6 collective-permute-done.5.refs_2_
  56.0 0.2 collective-permute-done.4.refs_1_
  56.2 0.2 merge.5.refs_2_
  56.4 0.0 copy-done
  56.4 4.0 %back.1 = bf16[32,80,128]{2,1,0:T(8,128)(2,1)S(1)} custom-call(f32[64,4096]{1,0:T(8,128)S(1)} %get-tuple-element.18.field_ref, bf16[9,32,4096]{2,1,0:T(8,128)(2,1)S(1)} %copy-done, s32[64,128]{1,0:T(8,128)S(1)} %get-tuple-element.19.spot_ref, bf16[64,32]{1,0:T(8,128)(2,1)S(1)} %get-tuple-element.21.refs_0_, bf16[64,64]{1,0:T(8,128)(2,1)S(1)} %get-tuple-element.23.refs_1_, ...), custom_call_target="tpu_custom_call" | custom-call | flops 1073741824 | bytes 1048576 | tf_op jit(solution)/shard_map/back/pallas_call | solution.py:496
  60.4 21.3 %all_to_all.11.ret_ref = bf16[32,80,128]{2,1,0:T(8,128)(2,1)S(1)} all-to-all(bf16[32,80,128]{2,1,0:T(8,128)(2,1)S(1)} %back.1), channel_id=1, replica_groups=mesh['leaf'=8,'sub'=4] {'leaf','sub'}, dimensions={0} | all-to-all | bytes 1310720 | tf_op jit(solution)/shard_map/all_to_all | solution.py:445
  81.7 5.5 %final.1 = bf16[64,5120]{1,0:T(8,128)(2,1)} custom-call(bf16[32,80,128]{2,1,0:T(8,128)(2,1)S(1)} %all_to_all.11.ret_ref, s32[40,128]{1,0:T(8,128)S(1)} %get-tuple-element.25.row_ref, s32[40,128]{1,0:T(8,128)S(1)} %get-tuple-element.26.part_ref), custom_call_target="tpu_custom_call" | custom-call | flops 1073741824 | bytes 1048576 | tf_op jit(solution)/shard_map/final/pallas_call | solution.py:512
Async XLA Ops:
  33.9 22.5 %copy-start = (bf16[9,32,4096]{2,1,0:T(8,128)(2,1)S(1)}, bf16[9,32,4096]{2,1,0:T(8,128)(2,1)}, u32[]{:S(2)}) copy-start(bf16[9,32,4096]{2,1,0:T(8,128)(2,1)} %left.1) | copy-start | bytes 7077892
  40.9 1.3 %collective-permute-start = (bf16[160,128]{1,0:T(8,128)(2,1)S(1)}, bf16[160,128]{1,0:T(8,128)(2,1)S(1)}, u32[]{:S(2)}, u32[]{:S(2)}) collective-permute-start(bf16[160,128]{1,0:T(8,128)(2,1)S(1)} %get-tuple-element.20.refs_0_), channel_id=1, source_target_pairs={{0,1},{1,0},{2,3},{3,2},{4,5},{5,4},{6,7},{7,6},{8,9},{9,8},{10,11... | collective-permute-start | bytes 122888 | tf_op jit(solution)/shard_map/ppermute | solution.py:390
  42.5 4.9 %collective-permute-start.3 = (bf16[128,128]{1,0:T(8,128)(2,1)S(1)}, bf16[128,128]{1,0:T(8,128)(2,1)S(1)}, u32[]{:S(2)}, u32[]{:S(2)}) collective-permute-start(bf16[128,128]{1,0:T(8,128)(2,1)S(1)} %get-tuple-element.22.refs_0_), channel_id=1, source_target_pairs={{0,6},{1,7},{2,4},{3,5},{4,2},{5,3},{6,0},{7,1},{8,14},{9,15},{10,... | collective-permute-start | bytes 98312 | tf_op jit(solution)/shard_map/ppermute | solution.py:390
  44.9 3.9 %collective-permute-start.2 = (bf16[128,128]{1,0:T(8,128)(2,1)S(1)}, bf16[128,128]{1,0:T(8,128)(2,1)S(1)}, u32[]{:S(2)}, u32[]{:S(2)}) collective-permute-start(bf16[128,128]{1,0:T(8,128)(2,1)S(1)} %get-tuple-element.22.refs_0_), channel_id=1, source_target_pairs={{0,4},{1,5},{2,6},{3,7},{4,0},{5,1},{6,2},{7,3},{8,12},{9,13},{10,... | collective-permute-start | bytes 98312 | tf_op jit(solution)/shard_map/ppermute | solution.py:390
  45.5 3.9 %collective-permute-start.1 = (bf16[128,128]{1,0:T(8,128)(2,1)S(1)}, bf16[128,128]{1,0:T(8,128)(2,1)S(1)}, u32[]{:S(2)}, u32[]{:S(2)}) collective-permute-start(bf16[128,128]{1,0:T(8,128)(2,1)S(1)} %get-tuple-element.22.refs_0_), channel_id=1, source_target_pairs={{0,2},{1,3},{2,0},{3,1},{4,6},{5,7},{6,4},{7,5},{8,10},{9,11},{10,... | collective-permute-start | bytes 98312 | tf_op jit(solution)/shard_map/ppermute | solution.py:390
  49.9 5.6 %collective-permute-start.6 = (bf16[64,128]{1,0:T(8,128)(2,1)S(1)}, bf16[64,128]{1,0:T(8,128)(2,1)S(1)}, u32[]{:S(2)}, u32[]{:S(2)}) collective-permute-start(bf16[64,128]{1,0:T(8,128)(2,1)S(1)} %get-tuple-element.24.refs_0_), channel_id=1, source_target_pairs={{0,24},{1,25},{2,26},{3,27},{4,28},{5,29},{6,30},{7,31},{8,16},{9,... | collective-permute-start | bytes 49160 | tf_op jit(solution)/shard_map/ppermute | solution.py:390
  51.4 4.6 %collective-permute-start.5 = (bf16[64,128]{1,0:T(8,128)(2,1)S(1)}, bf16[64,128]{1,0:T(8,128)(2,1)S(1)}, u32[]{:S(2)}, u32[]{:S(2)}) collective-permute-start(bf16[64,128]{1,0:T(8,128)(2,1)S(1)} %get-tuple-element.24.refs_0_), channel_id=1, source_target_pairs={{0,16},{1,17},{2,18},{3,19},{4,20},{5,21},{6,22},{7,23},{8,24},{9,... | collective-permute-start | bytes 49160 | tf_op jit(solution)/shard_map/ppermute | solution.py:390
  52.1 4.1 %collective-permute-start.4 = (bf16[64,128]{1,0:T(8,128)(2,1)S(1)}, bf16[64,128]{1,0:T(8,128)(2,1)S(1)}, u32[]{:S(2)}, u32[]{:S(2)}) collective-permute-start(bf16[64,128]{1,0:T(8,128)(2,1)S(1)} %get-tuple-element.24.refs_0_), channel_id=1, source_target_pairs={{0,8},{1,9},{2,10},{3,11},{4,12},{5,13},{6,14},{7,15},{8,0},{9,1},... | collective-permute-start | bytes 49160 | tf_op jit(solution)/shard_map/ppermute | solution.py:390

commit v2 on v1

--- a/solution.py
+++ b/solution.py
@@ -16,10 +16,10 @@
 NT = (((1,), (1,)), ((), ()))
 VMEM = pltpu.VMEM
 SMEM = pltpu.SMEM
-FINAL_UNROLL = 40
+SEGMENTS = 8
 PLACE_UNROLL = 32
 PICK_UNROLL = 32
-SEND_UNROLL = 1
+SEND_UNROLL = 40
 
 
 def dot(a, b):
@@ -41,7 +41,7 @@
 def send_kernel(
     rows, vecs, half, n_sub, first, counts_hbm, vec_hbm, slot_hbm, left_hbm, right_hbm,
     out_ref, row_ref, part_ref, gram_ref,
-    counts, vec, slots, left, right, xt, staged, flat, places, owners, codes, pos, posf, sems,
+    counts, vec, slots, left, right, xt, staged, flat, places, owners, codes, posf, sems,
 ):
     devices = out_ref.shape[0]
     parts = LANES // vecs
@@ -63,10 +63,12 @@
     before = (iota((LANES, LANES), 0) < iota((LANES, LANES), 1)).astype(BF16)
     ones = jnp.ones((LANES, LANES), BF16)
     carry = jnp.zeros((devices, LANES), F32)
-    loads[0].wait()
-    loads[1].wait()
+    for load in loads[:3]:
+        load.wait()
     count = counts[lax.axis_index("leaf") * n_sub + lax.axis_index("sub")]
     for b in range(blocks):
+        x = vec[:, b * LANES : (b + 1) * LANES].astype(F32)
+        xt[b * LANES : (b + 1) * LANES, :] = jnp.concatenate([x] * parts, axis=0).T
         slot = slots[b : b + 1, :]
         lane = iota((1, LANES), 1) + b * LANES
         live = (lane < count) & (slot >= 0)
@@ -87,54 +89,42 @@
         codes[b : b + 1, :] = part * LANES + inner
     copy = pltpu.make_async_copy(flat, places, sems.at[5])
     copy.start()
-    for load in loads[2:]:
+    for load in loads[3:]:
         load.wait()
-    pos[...] = jnp.zeros(pos.shape, F32)
-    gram_ref[...] = jnp.zeros(gram_ref.shape, F32)
     code_id = iota((parts * LANES, LANES), 0)
-    tile = 256
-    tiles = rows // tile
-
-    def turn(b, _):
-        at = pl.multiple_of(b * LANES, LANES)
-        x = vec[:, pl.ds(at, LANES)].astype(F32)
-        xt[pl.ds(at, LANES), :] = jnp.concatenate([x] * parts, axis=0).T
-        return 0
-
-    lax.fori_loop(0, blocks, turn, 0, unroll=8)
-    copy.wait()
-
-    def move(i, _):
+
+    total = jnp.zeros((2 * devices, parts * LANES), F32)
+    for i in range(blocks // 2):
         digits, spread = [], []
-        for s in range(2):
-            b = 2 * i + s
-            hot = owner_id == owners[pl.ds(b, 1), :]
-            local = slots[pl.ds(b, 1), :] & (rows - 1)
+        for b in (2 * i, 2 * i + 1):
+            hot = owner_id == owners[b : b + 1, :]
+            local = slots[b : b + 1, :] & (rows - 1)
             high = ((local >> 6) + 1).astype(F32)
             low = (local & (DIGIT - 1)).astype(F32)
             digits.append(
                 jnp.concatenate([jnp.where(hot, high, 0.0), jnp.where(hot, low, 0.0)], axis=0)
             )
-            spread.append(jnp.where(code_id == codes[pl.ds(b, 1), :], 1.0, 0.0))
-            for u in range(LANES):
-                staged[pl.ds(places[b, u], 1), :] = xt[pl.ds(b * LANES + u, 1), :]
-        pos[...] = pos[...] + dot_nt(
+            spread.append(jnp.where(code_id == codes[b : b + 1, :], 1.0, 0.0))
+        total = total + dot_nt(
             jnp.concatenate(digits, axis=1).astype(BF16),
             jnp.concatenate(spread, axis=1).astype(BF16),
         )
-        at = pl.ds(pl.multiple_of(jnp.minimum(i, tiles - 1) * tile, tile), tile)
-        keep = jnp.where(i < tiles, 1.0, 0.0)
-        lhs = jnp.concatenate([left[k, :, at] for k in range(cross)], axis=0)
-        rhs = jnp.concatenate([right[k, :, at] for k in range(cross)], axis=0)
-        gram_ref[...] = gram_ref[...] + dot_nt(lhs, rhs) * keep
-        return 0
-
-    lax.fori_loop(0, blocks // 2, move, 0, unroll=SEND_UNROLL)
     for d in range(devices):
         for q in range(parts):
             at = slice(q * LANES, (q + 1) * LANES)
-            posf[8 * d + q : 8 * d + q + 1, :] = pos[d : d + 1, at]
-            posf[8 * d + parts + q : 8 * d + parts + q + 1, :] = pos[devices + d : devices + d + 1, at]
+            posf[8 * d + q : 8 * d + q + 1, :] = total[d : d + 1, at]
+            posf[8 * d + parts + q : 8 * d + parts + q + 1, :] = total[devices + d : devices + d + 1, at]
+    lhs = jnp.concatenate([left[k] for k in range(cross - 1)], axis=0)
+    rhs = jnp.concatenate([right[k] for k in range(1, cross)], axis=0)
+    gram_ref[...] = dot_nt(lhs, rhs)
+    copy.wait()
+
+    def move(b, _):
+        for u in range(LANES):
+            staged[pl.ds(places[b, u], 1), :] = xt[pl.ds(b * LANES + u, 1), :]
+        return 0
+
+    lax.fori_loop(0, blocks, move, 0, unroll=SEND_UNROLL)
     group = iota((half, LANES), 1) // vecs
 
     def pack(d, _):
@@ -259,44 +249,56 @@
             field_ref[:, at] = field_ref[:, at] - dot(coeff[n ^ 1], left[k, :, at])
     rounded = field_ref[...].astype(BF16)
     cross = levels - local_levels
-    b = jnp.concatenate([dot_nt(rounded, right[k]) for k in range(local_levels, levels)], axis=1)
-    gram = [gram_ref[j * rank : (j + 1) * rank, :] for j in range(cross)]
+    b = dot_nt(rounded, jnp.concatenate([right[k] for k in range(local_levels, levels)], axis=0))
+    blank = jnp.zeros((rank, rank), F32)
+    gram = [
+        jnp.concatenate([blank, gram_ref[j * rank : (j + 1) * rank, :]], axis=1)
+        for j in range(cross - 1)
+    ]
     pack_bands(message_ref, b, gram, rank, vecs // rank, cross)
 
 
-def merge_kernel(bits, rank, scales, vecs, levels, *refs):
-    group = 1 << bits
-    p_ref = refs[group]
+def merge(messages, rank, scales, vecs, levels):
     halves = vecs // rank
-    found = [unpack_bands(r[...].astype(F32), rank, halves, levels) for r in refs[:group]]
+    found = [unpack_bands(m.astype(F32), rank, halves, levels) for m in messages]
     b = [f[0] for f in found]
     gram = [f[1] for f in found]
-    for step in range(bits):
+    solved = []
+    for step, scale in enumerate(scales):
         at = slice(step * rank, (step + 1) * rank)
-        p = [(b[x ^ 1][:, at] * scales[step]).astype(BF16) for x in range(len(b))]
-        p_ref[:, at] = p[0]
+        p = [(b[x ^ 1][:, at] * scale).astype(BF16) for x in range(len(b))]
+        solved.append(p[0])
         if step + 1 < levels:
             b = [b[x] - dot(p[x], gram[x][step].astype(BF16)) for x in range(len(b))]
             b = [b[x] + b[x + 1] for x in range(0, len(b), 2)]
             gram = [
                 [u + v for u, v in zip(gram[x], gram[x + 1])] for x in range(0, len(gram), 2)
             ]
-    if levels > bits:
-        keep = slice(bits * rank, levels * rank)
-        rest = [g[:, keep] for g in gram[0][bits:]]
-        pack_bands(refs[group + 1], b[0][:, keep], rest, rank, halves, levels - bits)
-
-
-def back_kernel(first, rank, n_solved, field_ref, left, spot_ref, *refs):
-    solved = refs[:n_solved]
-    out_ref, done, spots, packed, sem = refs[n_solved:]
+    return solved, b[0], gram[0]
+
+
+def merge_kernel(rank, scales, vecs, levels, *refs):
+    bits = len(scales)
+    messages, (p_ref, out_ref) = refs[:-2], refs[-2:]
+    solved, b, gram = merge([r[...] for r in messages], rank, scales, vecs, levels)
+    for step in range(bits):
+        p_ref[:, step * rank : (step + 1) * rank] = solved[step]
+    keep = slice(bits * rank, levels * rank)
+    rest = [g[:, keep] for g in gram[bits:]]
+    pack_bands(out_ref, b[:, keep], rest, rank, vecs // rank, levels - bits)
+
+
+def back_kernel(first, rank, scales, n_solved, field_ref, left, spot_ref, *refs):
+    out_ref, done, spots, packed, sem = refs[-5:]
+    messages = [r[...] for r in refs[n_solved:-5]]
     devices, half, _ = out_ref.shape
     vecs, rows = field_ref.shape
     parts = LANES // vecs
     levels = left.shape[0]
     copy = pltpu.make_async_copy(spot_ref, spots, sem)
     copy.start()
-    p = jnp.concatenate([r[...] for r in solved], axis=1)
+    last = merge(messages, rank, scales, vecs, len(scales))[0]
+    p = jnp.concatenate([r[...] for r in refs[:n_solved]] + last, axis=1)
     wide = 512
     for c in range(rows // wide):
         at = slice(c * wide, (c + 1) * wide)
@@ -326,12 +328,12 @@
     lax.fori_loop(0, devices, narrow, 0)
 
 
-def final_kernel(ret_ref, row_ref, part_ref, out_ref, ret, picked, places, sem):
+def final_kernel(segments, ret_ref, row_ref, part_ref, out_hbm, ret, picked, out, places, sems):
     devices, half, _ = ret_ref.shape
-    vecs = out_ref.shape[0]
+    vecs = out.shape[0]
     parts = LANES // vecs
     blocks = row_ref.shape[0]
-    copy = pltpu.make_async_copy(row_ref, places, sem)
+    copy = pltpu.make_async_copy(row_ref, places, sems.at[segments])
     copy.start()
 
     def widen(d, _):
@@ -346,14 +348,28 @@
             picked[pl.ds(b * LANES + u, 1), :] = ret[pl.ds(places[b, u], 1), :]
         return 0
 
-    lax.fori_loop(0, blocks, move, 0, unroll=FINAL_UNROLL)
-    for b in range(blocks):
+    def turn(b):
         x = picked[b * LANES : (b + 1) * LANES, :].T
         part = part_ref[b : b + 1, :]
-        value = jnp.zeros((vecs, LANES), F32)
-        for q in range(parts):
+        value = x[:vecs]
+        for q in range(1, parts):
             value = jnp.where(part == q, x[q * vecs : (q + 1) * vecs], value)
-        out_ref[:, b * LANES : (b + 1) * LANES] = value.astype(BF16)
+        value = jnp.where(part == parts, 0.0, value)
+        out[:, b * LANES : (b + 1) * LANES] = value.astype(BF16)
+
+    per = blocks // segments
+    stores = []
+    for g in range(segments + 1):
+        if g < segments:
+            lax.fori_loop(g * per, (g + 1) * per, move, 0, unroll=per)
+        if g > 0:
+            for b in range((g - 1) * per, g * per):
+                turn(b)
+            at = pl.ds((g - 1) * per * LANES, per * LANES)
+            stores.append(pltpu.make_async_copy(out.at[:, at], out_hbm.at[:, at], sems.at[g - 1]))
+            stores[-1].start()
+    for store in stores:
+        store.wait()
 
 
 def full(shape, dtype):
@@ -419,7 +435,7 @@
             full((devices, half + 8, LANES), BF16),
             full((blocks, LANES), I32),
             full((blocks, LANES), I32),
-            full((cross * rank, cross * rank), F32),
+            full(((cross - 1) * rank, (cross - 1) * rank), F32),
         ),
         [hbm()] * 5,
         (vmem(),) * 4,
@@ -435,7 +451,6 @@
             SMEM((blocks, LANES), I32),
             VMEM((blocks, LANES), I32),
             VMEM((blocks, LANES), I32),
-            VMEM((2 * devices, parts * LANES), F32),
             VMEM((8 * devices, LANES), F32),
             pltpu.SemaphoreType.DMA((6,)),
         ],
@@ -477,29 +492,30 @@
         group = [message] + [flipped(message, axes, m << bit) for m in range(1, 1 << take)]
         scales = [1.0 / math.sqrt(leaf << (level + s)) for s in range(take)]
         left_over = cross - bit - take
-        shapes = [full((vecs, take * rank), BF16)]
-        if left_over:
-            shapes.append(full((band_rows(halves, left_over, rank), LANES), BF16))
-        out = call(
-            functools.partial(merge_kernel, take, rank, scales, vecs, cross - bit),
+        bit += take
+        if not left_over:
+            break
+        p, message = call(
+            functools.partial(merge_kernel, rank, scales, vecs, left_over + take),
             "merge",
             4,
             1 << 24,
-            tuple(shapes),
+            (
+                full((vecs, take * rank), BF16),
+                full((band_rows(halves, left_over, rank), LANES), BF16),
+            ),
             [vmem()] * len(group),
-            (vmem(),) * len(shapes),
+            (vmem(),) * 2,
         )(*group)
-        solved.append(out[0])
-        message = out[-1]
-        bit += take
+        solved.append(p)
 
     back = call(
-        functools.partial(back_kernel, local_levels, rank, len(solved)),
+        functools.partial(back_kernel, local_levels, rank, scales, len(solved)),
         "back",
         14,
         1 << 30,
         full((devices, half, LANES), BF16),
-        [vmem()] * (3 + len(solved)),
+        [vmem()] * (3 + len(solved) + len(group)),
         vmem(),
         [
             VMEM((rows + 8, LANES), F32),
@@ -507,21 +523,23 @@
             VMEM((devices * half, LANES), F32),
             pltpu.SemaphoreType.DMA,
         ],
-    )(field, left_basis, spots, *solved)
+    )(field, left_basis, spots, *solved, *group)
     returned = exchange(back)
+    segments = SEGMENTS if blocks % SEGMENTS == 0 else 1
     return call(
-        final_kernel,
+        functools.partial(final_kernel, segments),
         "final",
         14,
         1 << 30,
         full((vecs, slots), BF16),
         [vmem(), vmem(), vmem()],
-        vmem(),
+        hbm(),
         [
             VMEM((devices * half, LANES), F32),
             VMEM((slots, LANES), F32),
+            VMEM((vecs, slots), BF16),
             SMEM((blocks, LANES), I32),
-            pltpu.SemaphoreType.DMA,
+            pltpu.SemaphoreType.DMA((segments + 1,)),
         ],
     )(returned, row_of, part_of)
 

time: 87.5 us -> 86.1 us (0.984)
  Pallas kernels: 25 us -> 23.6 us
    pallas_call x1, Pallas kernels: 7.58 us -> 6.18 us  [body(): call(functools.partial(send_kernel, rows, vecs, half, n_sub, local_levels...]
    pallas_call x5 -> x4, Pallas kernels: 10.4 us -> 10.3 us  [the longest x1 5.33 us: body(): call(functools.partial(final_kernel, segments), 'final', 14, 1 << 30, ful...]
where the time goes in v2:
time: 86.1 us; the launch traced here: 85.9 us
  blocking collectives  47.6 us (55%)
  Pallas kernels  23.6 us (27%)
  starting transfers between devices  8.15 us (9%)
  waiting for transfers between devices  6.35 us (7%)
    all_to_all x2, blocking collectives, exchange(): return lax.all_to_all(x, axes, split_axis=0, concat_axis=0, tiled=True)  47.6 us
    ppermute x7, starting transfers between devices, flipped(): return lax.ppermute(block, axes, [(i, i ^ mask) for i in range(count)])  8.15 us
    pallas_call x1, Pallas kernels, body(): call(functools.partial(tree_kernel, local_levels, leaf, rank), 'tree', 20...  7.08 us
    ppermute x7, waiting for transfers between devices, flipped(): return lax.ppermute(block, axes, [(i, i ^ mask) for i in range(count)])  6.35 us
    pallas_call x1, Pallas kernels, body(): call(functools.partial(send_kernel, rows, vecs, half, n_sub, local_levels...  6.18 us
    pallas_call x1, Pallas kernels, body(): call(functools.partial(final_kernel, segments), 'final', 14, 1 << 30, ful...  5.33 us
    pallas_call x1, Pallas kernels, body(): call(functools.partial(back_kernel, local_levels, rank, scales, len(solve...  4.18 us
  transfers between devices with their start and end apart: 7, of which 7 were waited for; matrix products, arithmetic and copies ran while one was open for 0% of the time, Pallas kernels for 0%

profile of v2, /device:TPU:0, one launch (start us, length us, event | category | flops | bytes accessed | tf_op | source)
XLA Modules:
  0.0 85.9 jit_solution(515339921822457393)
XLA Ops:
  0.0 6.2 %send.1 = (bf16[32,88,128]{2,1,0:T(8,128)(2,1)S(1)}, s32[40,128]{1,0:T(8,128)S(1)}, s32[40,128]{1,0:T(8,128)S(1)}, f32[128,128]{1,0:T(8,128)S(1)}) custom-call(s32[32]{0:T(128)} %counts_hbm.1, bf16[64,5120]{1,0:T(8,128)(2,1)} %vec_hbm.1, s32[40,128]{1,0:T(8,128)} %bitcast.1, bf16[9,32,4096]{2,1,0:T(8,128)(2,1)} %left.1, bf16[9,32,4096]{2,1,0:T(8,128)(2,1)} %right_hbm.3), custom_call_target="tpu_custom_call" | custom-call | flops 1073741824 | bytes 1048576 | tf_op jit(solution)/shard_map/send/pallas_call | solution.py:429
  6.2 26.3 %all_to_all.10.arr_ref = bf16[32,88,128]{2,1,0:T(8,128)(2,1)S(1)} all-to-all(bf16[32,88,128]{2,1,0:T(8,128)(2,1)S(1)} %get-tuple-element.16), channel_id=1, replica_groups=mesh['leaf'=8,'sub'=4] {'leaf','sub'}, dimensions={0} | all-to-all | bytes 1441792 | tf_op jit(solution)/shard_map/all_to_all | solution.py:460
  32.5 0.0 copy-start
  32.5 7.1 %tree.1 = (f32[64,4096]{1,0:T(8,128)S(1)}, bf16[160,128]{1,0:T(8,128)(2,1)S(1)}, s32[64,128]{1,0:T(8,128)S(1)}) custom-call(bf16[32,88,128]{2,1,0:T(8,128)(2,1)S(1)} %all_to_all.10.arr_ref, bf16[16,256,256]{2,1,0:T(8,128)(2,1)} %inv_hbm.1, bf16[9,32,4096]{2,1,0:T(8,128)(2,1)} %left.1, bf16[9,32,4096]{2,1,0:T(8,128)(2,1)} %right_hbm.3, ...), custom_call_target="tpu_custom_call" | custom-call | flops 1073741824 | bytes 1048576 | tf_op jit(solution)/shard_map/tree/pallas_call | solution.py:464
  39.6 0.2 collective-permute-start
  39.8 1.1 %collective-permute-done.refs_1_ = bf16[160,128]{1,0:T(8,128)(2,1)S(1)} collective-permute-done((bf16[160,128]{1,0:T(8,128)(2,1)S(1)}, bf16[160,128]{1,0:T(8,128)(2,1)S(1)}, u32[]{:S(2)}, u32[]{:S(2)}) %collective-permute-start) | collective-permute-done | bytes 40992 | tf_op jit(solution)/shard_map/ppermute | solution.py:406
  40.9 0.3 merge.2
  41.2 2.5 %collective-permute-start.3 = (bf16[128,128]{1,0:T(8,128)(2,1)S(1)}, bf16[128,128]{1,0:T(8,128)(2,1)S(1)}, u32[]{:S(2)}, u32[]{:S(2)}) collective-permute-start(bf16[128,128]{1,0:T(8,128)(2,1)S(1)} %get-tuple-element.22.refs_0_), channel_id=1, source_target_pairs={{0,6},{1,7},{2,4},{3,5},{4,2},{5,3},{6,0},{7,1},{8,14},{9,15},{10,... | collective-permute-start | bytes 98312 | tf_op jit(solution)/shard_map/ppermute | solution.py:406
  43.6 0.5 collective-permute-start.2
  44.2 0.5 collective-permute-start.1
  44.7 1.3 %collective-permute-done.3.refs_3_ = bf16[128,128]{1,0:T(8,128)(2,1)S(1)} collective-permute-done((bf16[128,128]{1,0:T(8,128)(2,1)S(1)}, bf16[128,128]{1,0:T(8,128)(2,1)S(1)}, u32[]{:S(2)}, u32[]{:S(2)}) %collective-permute-start.3) | collective-permute-done | bytes 32800 | tf_op jit(solution)/shard_map/ppermute | solution.py:406
  46.0 1.5 %collective-permute-done.2.refs_2_ = bf16[128,128]{1,0:T(8,128)(2,1)S(1)} collective-permute-done((bf16[128,128]{1,0:T(8,128)(2,1)S(1)}, bf16[128,128]{1,0:T(8,128)(2,1)S(1)}, u32[]{:S(2)}, u32[]{:S(2)}) %collective-permute-start.2) | collective-permute-done | bytes 32800 | tf_op jit(solution)/shard_map/ppermute | solution.py:406
  47.6 0.5 collective-permute-done.1.refs_1_
  48.1 0.5 merge.3
  48.6 1.5 %collective-permute-start.6 = (bf16[64,128]{1,0:T(8,128)(2,1)S(1)}, bf16[64,128]{1,0:T(8,128)(2,1)S(1)}, u32[]{:S(2)}, u32[]{:S(2)}) collective-permute-start(bf16[64,128]{1,0:T(8,128)(2,1)S(1)} %get-tuple-element.24.refs_2_), channel_id=1, source_target_pairs={{0,24},{1,25},{2,26},{3,27},{4,28},{5,29},{6,30},{7,31},{8,16},{9,... | collective-permute-start | bytes 49160 | tf_op jit(solution)/shard_map/ppermute | solution.py:406
  50.1 0.7 collective-permute-start.5
  50.8 2.2 %collective-permute-start.4 = (bf16[64,128]{1,0:T(8,128)(2,1)S(1)}, bf16[64,128]{1,0:T(8,128)(2,1)S(1)}, u32[]{:S(2)}, u32[]{:S(2)}) collective-permute-start(bf16[64,128]{1,0:T(8,128)(2,1)S(1)} %get-tuple-element.24.refs_2_), channel_id=1, source_target_pairs={{0,8},{1,9},{2,10},{3,11},{4,12},{5,13},{6,14},{7,15},{8,0},{9,1},... | collective-permute-start | bytes 49160 | tf_op jit(solution)/shard_map/ppermute | solution.py:406
  53.0 1.1 %collective-permute-done.6.refs_5_ = bf16[64,128]{1,0:T(8,128)(2,1)S(1)} collective-permute-done((bf16[64,128]{1,0:T(8,128)(2,1)S(1)}, bf16[64,128]{1,0:T(8,128)(2,1)S(1)}, u32[]{:S(2)}, u32[]{:S(2)}) %collective-permute-start.6) | collective-permute-done | bytes 16416 | tf_op jit(solution)/shard_map/ppermute | solution.py:406
  54.2 0.6 collective-permute-done.5.refs_4_
  54.7 0.2 collective-permute-done.4.refs_3_
  54.9 0.0 copy-done
  54.9 4.2 %back.1 = bf16[32,80,128]{2,1,0:T(8,128)(2,1)S(1)} custom-call(f32[64,4096]{1,0:T(8,128)S(1)} %get-tuple-element.18.field_ref, bf16[9,32,4096]{2,1,0:T(8,128)(2,1)S(1)} %copy-done, s32[64,128]{1,0:T(8,128)S(1)} %get-tuple-element.19.spot_ref, bf16[64,32]{1,0:T(8,128)(2,1)S(1)} %get-tuple-element.21.refs_0_, bf16[64,64]{1,0:T(8,128)(2,1)S(1)} %get-tuple-element.23.refs_1_, ...), custom_call_target="tpu_custom_call" | custom-call | flops 1073741824 | bytes 1048576 | tf_op jit(solution)/shard_map/back/pallas_call | solution.py:512
  59.1 21.3 %all_to_all.11.ret_ref = bf16[32,80,128]{2,1,0:T(8,128)(2,1)S(1)} all-to-all(bf16[32,80,128]{2,1,0:T(8,128)(2,1)S(1)} %back.1), channel_id=1, replica_groups=mesh['leaf'=8,'sub'=4] {'leaf','sub'}, dimensions={0} | all-to-all | bytes 1310720 | tf_op jit(solution)/shard_map/all_to_all | solution.py:460
  80.4 5.3 %final.1 = bf16[64,5120]{1,0:T(8,128)(2,1)} custom-call(bf16[32,80,128]{2,1,0:T(8,128)(2,1)S(1)} %all_to_all.11.ret_ref, s32[40,128]{1,0:T(8,128)S(1)} %get-tuple-element.25.row_ref, s32[40,128]{1,0:T(8,128)S(1)} %get-tuple-element.26.part_ref), custom_call_target="tpu_custom_call" | custom-call | flops 1073741824 | bytes 1048576 | tf_op jit(solution)/shard_map/final/pallas_call | solution.py:529
Async XLA Ops:
  32.5 22.4 %copy-start = (bf16[9,32,4096]{2,1,0:T(8,128)(2,1)S(1)}, bf16[9,32,4096]{2,1,0:T(8,128)(2,1)}, u32[]{:S(2)}) copy-start(bf16[9,32,4096]{2,1,0:T(8,128)(2,1)} %left.1) | copy-start | bytes 7077892
  39.6 1.3 %collective-permute-start = (bf16[160,128]{1,0:T(8,128)(2,1)S(1)}, bf16[160,128]{1,0:T(8,128)(2,1)S(1)}, u32[]{:S(2)}, u32[]{:S(2)}) collective-permute-start(bf16[160,128]{1,0:T(8,128)(2,1)S(1)} %get-tuple-element.20.refs_0_), channel_id=1, source_target_pairs={{0,1},{1,0},{2,3},{3,2},{4,5},{5,4},{6,7},{7,6},{8,9},{9,8},{10,11... | collective-permute-start | bytes 122888 | tf_op jit(solution)/shard_map/ppermute | solution.py:406
  41.2 4.9 %collective-permute-start.3 = (bf16[128,128]{1,0:T(8,128)(2,1)S(1)}, bf16[128,128]{1,0:T(8,128)(2,1)S(1)}, u32[]{:S(2)}, u32[]{:S(2)}) collective-permute-start(bf16[128,128]{1,0:T(8,128)(2,1)S(1)} %get-tuple-element.22.refs_0_), channel_id=1, source_target_pairs={{0,6},{1,7},{2,4},{3,5},{4,2},{5,3},{6,0},{7,1},{8,14},{9,15},{10,... | collective-permute-start | bytes 98312 | tf_op jit(solution)/shard_map/ppermute | solution.py:406
  43.6 3.9 %collective-permute-start.2 = (bf16[128,128]{1,0:T(8,128)(2,1)S(1)}, bf16[128,128]{1,0:T(8,128)(2,1)S(1)}, u32[]{:S(2)}, u32[]{:S(2)}) collective-permute-start(bf16[128,128]{1,0:T(8,128)(2,1)S(1)} %get-tuple-element.22.refs_0_), channel_id=1, source_target_pairs={{0,4},{1,5},{2,6},{3,7},{4,0},{5,1},{6,2},{7,3},{8,12},{9,13},{10,... | collective-permute-start | bytes 98312 | tf_op jit(solution)/shard_map/ppermute | solution.py:406
  44.2 3.9 %collective-permute-start.1 = (bf16[128,128]{1,0:T(8,128)(2,1)S(1)}, bf16[128,128]{1,0:T(8,128)(2,1)S(1)}, u32[]{:S(2)}, u32[]{:S(2)}) collective-permute-start(bf16[128,128]{1,0:T(8,128)(2,1)S(1)} %get-tuple-element.22.refs_0_), channel_id=1, source_target_pairs={{0,2},{1,3},{2,0},{3,1},{4,6},{5,7},{6,4},{7,5},{8,10},{9,11},{10,... | collective-permute-start | bytes 98312 | tf_op jit(solution)/shard_map/ppermute | solution.py:406
  48.6 5.6 %collective-permute-start.6 = (bf16[64,128]{1,0:T(8,128)(2,1)S(1)}, bf16[64,128]{1,0:T(8,128)(2,1)S(1)}, u32[]{:S(2)}, u32[]{:S(2)}) collective-permute-start(bf16[64,128]{1,0:T(8,128)(2,1)S(1)} %get-tuple-element.24.refs_2_), channel_id=1, source_target_pairs={{0,24},{1,25},{2,26},{3,27},{4,28},{5,29},{6,30},{7,31},{8,16},{9,... | collective-permute-start | bytes 49160 | tf_op jit(solution)/shard_map/ppermute | solution.py:406
  50.1 4.6 %collective-permute-start.5 = (bf16[64,128]{1,0:T(8,128)(2,1)S(1)}, bf16[64,128]{1,0:T(8,128)(2,1)S(1)}, u32[]{:S(2)}, u32[]{:S(2)}) collective-permute-start(bf16[64,128]{1,0:T(8,128)(2,1)S(1)} %get-tuple-element.24.refs_2_), channel_id=1, source_target_pairs={{0,16},{1,17},{2,18},{3,19},{4,20},{5,21},{6,22},{7,23},{8,24},{9,... | collective-permute-start | bytes 49160 | tf_op jit(solution)/shard_map/ppermute | solution.py:406
  50.8 4.1 %collective-permute-start.4 = (bf16[64,128]{1,0:T(8,128)(2,1)S(1)}, bf16[64,128]{1,0:T(8,128)(2,1)S(1)}, u32[]{:S(2)}, u32[]{:S(2)}) collective-permute-start(bf16[64,128]{1,0:T(8,128)(2,1)S(1)} %get-tuple-element.24.refs_2_), channel_id=1, source_target_pairs={{0,8},{1,9},{2,10},{3,11},{4,12},{5,13},{6,14},{7,15},{8,0},{9,1},... | collective-permute-start | bytes 49160 | tf_op jit(solution)/shard_map/ppermute | solution.py:406

commit v3 on v2

--- a/solution.py
+++ b/solution.py
@@ -181,7 +181,7 @@
 
 def tree_kernel(
     local_levels, leaf, rank, arr_ref, inv_hbm, left_hbm, right_hbm, gram_ref,
-    field_ref, message_ref, spot_ref, arr, tree, inv, left, right, spots, sems,
+    field_ref, message_ref, spot_ref, arr, tree, tree_rows, inv, left, right, spots, sems,
 ):
     devices = arr_ref.shape[0]
     vecs, rows = field_ref.shape
@@ -229,9 +229,12 @@
     lax.fori_loop(0, devices, place, 0, unroll=PLACE_UNROLL)
     for load in loads:
         load.wait()
+    products = tree_rows
     for l in range(leaves):
-        block = tree[l * leaf : (l + 1) * leaf, :].astype(BF16)
-        turned = dot(inv[l], block).T
+        at = slice(l * leaf, (l + 1) * leaf)
+        products[at, :] = dot(inv[l], tree[at, :].astype(BF16))
+    for l in range(leaves):
+        turned = products[l * leaf : (l + 1) * leaf, :].T
         total = turned[:vecs]
         for q in range(1, parts):
             total = total + turned[q * vecs : (q + 1) * vecs]
@@ -476,6 +479,7 @@
         [
             VMEM((devices * half, LANES), F32),
             VMEM((rows + 8, LANES), F32),
+            VMEM((rows, LANES), F32),
             VMEM((leaves, leaf, leaf), BF16),
             VMEM((local_levels, rank, rows), BF16),
             VMEM((levels, rank, rows), BF16),

time: 86.1 us -> 86.1 us (level)
  no operation moved by 1% of the time
where the time goes in v3:
time: 86.1 us; the launch traced here: 85.9 us
  blocking collectives  47.6 us (55%)
  Pallas kernels  23.6 us (27%)
  starting transfers between devices  8.15 us (9%)
  waiting for transfers between devices  6.35 us (7%)
    all_to_all x2, blocking collectives, exchange(): return lax.all_to_all(x, axes, split_axis=0, concat_axis=0, tiled=True)  47.6 us
    ppermute x7, starting transfers between devices, flipped(): return lax.ppermute(block, axes, [(i, i ^ mask) for i in range(count)])  8.15 us
    pallas_call x1, Pallas kernels, body(): call(functools.partial(tree_kernel, local_levels, leaf, rank), 'tree', 20...  7.07 us
    ppermute x7, waiting for transfers between devices, flipped(): return lax.ppermute(block, axes, [(i, i ^ mask) for i in range(count)])  6.35 us
    pallas_call x1, Pallas kernels, body(): call(functools.partial(send_kernel, rows, vecs, half, n_sub, local_levels...  6.18 us
    pallas_call x1, Pallas kernels, body(): call(functools.partial(final_kernel, segments), 'final', 14, 1 << 30, ful...  5.33 us
    pallas_call x1, Pallas kernels, body(): call(functools.partial(back_kernel, local_levels, rank, scales, len(solve...  4.18 us
  transfers between devices with their start and end apart: 7, of which 7 were waited for; matrix products, arithmetic and copies ran while one was open for 0% of the time, Pallas kernels for 0%

profile of v3, /device:TPU:0, one launch (start us, length us, event | category | flops | bytes accessed | tf_op | source)
XLA Modules:
  0.0 85.9 jit_solution(515339921822457393)
XLA Ops:
  0.0 6.2 %send.1 = (bf16[32,88,128]{2,1,0:T(8,128)(2,1)S(1)}, s32[40,128]{1,0:T(8,128)S(1)}, s32[40,128]{1,0:T(8,128)S(1)}, f32[128,128]{1,0:T(8,128)S(1)}) custom-call(s32[32]{0:T(128)} %counts_hbm.1, bf16[64,5120]{1,0:T(8,128)(2,1)} %vec_hbm.1, s32[40,128]{1,0:T(8,128)} %bitcast.1, bf16[9,32,4096]{2,1,0:T(8,128)(2,1)} %left.1, bf16[9,32,4096]{2,1,0:T(8,128)(2,1)} %right_hbm.3), custom_call_target="tpu_custom_call" | custom-call | flops 1073741824 | bytes 1048576 | tf_op jit(solution)/shard_map/send/pallas_call | solution.py:432
  6.2 26.3 %all_to_all.10.arr_ref = bf16[32,88,128]{2,1,0:T(8,128)(2,1)S(1)} all-to-all(bf16[32,88,128]{2,1,0:T(8,128)(2,1)S(1)} %get-tuple-element.16), channel_id=1, replica_groups=mesh['leaf'=8,'sub'=4] {'leaf','sub'}, dimensions={0} | all-to-all | bytes 1441792 | tf_op jit(solution)/shard_map/all_to_all | solution.py:463
  32.5 0.0 copy-start
  32.5 7.1 %tree.1 = (f32[64,4096]{1,0:T(8,128)S(1)}, bf16[160,128]{1,0:T(8,128)(2,1)S(1)}, s32[64,128]{1,0:T(8,128)S(1)}) custom-call(bf16[32,88,128]{2,1,0:T(8,128)(2,1)S(1)} %all_to_all.10.arr_ref, bf16[16,256,256]{2,1,0:T(8,128)(2,1)} %inv_hbm.1, bf16[9,32,4096]{2,1,0:T(8,128)(2,1)} %left.1, bf16[9,32,4096]{2,1,0:T(8,128)(2,1)} %right_hbm.3, ...), custom_call_target="tpu_custom_call" | custom-call | flops 1073741824 | bytes 1048576 | tf_op jit(solution)/shard_map/tree/pallas_call | solution.py:467
  39.6 0.2 collective-permute-start
  39.8 1.1 %collective-permute-done.refs_1_ = bf16[160,128]{1,0:T(8,128)(2,1)S(1)} collective-permute-done((bf16[160,128]{1,0:T(8,128)(2,1)S(1)}, bf16[160,128]{1,0:T(8,128)(2,1)S(1)}, u32[]{:S(2)}, u32[]{:S(2)}) %collective-permute-start) | collective-permute-done | bytes 40992 | tf_op jit(solution)/shard_map/ppermute | solution.py:409
  40.9 0.3 merge.2
  41.2 2.5 %collective-permute-start.3 = (bf16[128,128]{1,0:T(8,128)(2,1)S(1)}, bf16[128,128]{1,0:T(8,128)(2,1)S(1)}, u32[]{:S(2)}, u32[]{:S(2)}) collective-permute-start(bf16[128,128]{1,0:T(8,128)(2,1)S(1)} %get-tuple-element.22.refs_0_), channel_id=1, source_target_pairs={{0,6},{1,7},{2,4},{3,5},{4,2},{5,3},{6,0},{7,1},{8,14},{9,15},{10,... | collective-permute-start | bytes 98312 | tf_op jit(solution)/shard_map/ppermute | solution.py:409
  43.6 0.5 collective-permute-start.2
  44.2 0.5 collective-permute-start.1
  44.7 1.3 %collective-permute-done.3.refs_3_ = bf16[128,128]{1,0:T(8,128)(2,1)S(1)} collective-permute-done((bf16[128,128]{1,0:T(8,128)(2,1)S(1)}, bf16[128,128]{1,0:T(8,128)(2,1)S(1)}, u32[]{:S(2)}, u32[]{:S(2)}) %collective-permute-start.3) | collective-permute-done | bytes 32800 | tf_op jit(solution)/shard_map/ppermute | solution.py:409
  46.0 1.5 %collective-permute-done.2.refs_2_ = bf16[128,128]{1,0:T(8,128)(2,1)S(1)} collective-permute-done((bf16[128,128]{1,0:T(8,128)(2,1)S(1)}, bf16[128,128]{1,0:T(8,128)(2,1)S(1)}, u32[]{:S(2)}, u32[]{:S(2)}) %collective-permute-start.2) | collective-permute-done | bytes 32800 | tf_op jit(solution)/shard_map/ppermute | solution.py:409
  47.6 0.5 collective-permute-done.1.refs_1_
  48.1 0.5 merge.3
  48.6 1.5 %collective-permute-start.6 = (bf16[64,128]{1,0:T(8,128)(2,1)S(1)}, bf16[64,128]{1,0:T(8,128)(2,1)S(1)}, u32[]{:S(2)}, u32[]{:S(2)}) collective-permute-start(bf16[64,128]{1,0:T(8,128)(2,1)S(1)} %get-tuple-element.24.refs_2_), channel_id=1, source_target_pairs={{0,24},{1,25},{2,26},{3,27},{4,28},{5,29},{6,30},{7,31},{8,16},{9,... | collective-permute-start | bytes 49160 | tf_op jit(solution)/shard_map/ppermute | solution.py:409
  50.1 0.7 collective-permute-start.5
  50.8 2.2 %collective-permute-start.4 = (bf16[64,128]{1,0:T(8,128)(2,1)S(1)}, bf16[64,128]{1,0:T(8,128)(2,1)S(1)}, u32[]{:S(2)}, u32[]{:S(2)}) collective-permute-start(bf16[64,128]{1,0:T(8,128)(2,1)S(1)} %get-tuple-element.24.refs_2_), channel_id=1, source_target_pairs={{0,8},{1,9},{2,10},{3,11},{4,12},{5,13},{6,14},{7,15},{8,0},{9,1},... | collective-permute-start | bytes 49160 | tf_op jit(solution)/shard_map/ppermute | solution.py:409
  53.0 1.1 %collective-permute-done.6.refs_5_ = bf16[64,128]{1,0:T(8,128)(2,1)S(1)} collective-permute-done((bf16[64,128]{1,0:T(8,128)(2,1)S(1)}, bf16[64,128]{1,0:T(8,128)(2,1)S(1)}, u32[]{:S(2)}, u32[]{:S(2)}) %collective-permute-start.6) | collective-permute-done | bytes 16416 | tf_op jit(solution)/shard_map/ppermute | solution.py:409
  54.2 0.6 collective-permute-done.5.refs_4_
  54.7 0.2 collective-permute-done.4.refs_3_
  54.9 0.0 copy-done
  54.9 4.2 %back.1 = bf16[32,80,128]{2,1,0:T(8,128)(2,1)S(1)} custom-call(f32[64,4096]{1,0:T(8,128)S(1)} %get-tuple-element.18.field_ref, bf16[9,32,4096]{2,1,0:T(8,128)(2,1)S(1)} %copy-done, s32[64,128]{1,0:T(8,128)S(1)} %get-tuple-element.19.spot_ref, bf16[64,32]{1,0:T(8,128)(2,1)S(1)} %get-tuple-element.21.refs_0_, bf16[64,64]{1,0:T(8,128)(2,1)S(1)} %get-tuple-element.23.refs_1_, ...), custom_call_target="tpu_custom_call" | custom-call | flops 1073741824 | bytes 1048576 | tf_op jit(solution)/shard_map/back/pallas_call | solution.py:516
  59.1 21.3 %all_to_all.11.ret_ref = bf16[32,80,128]{2,1,0:T(8,128)(2,1)S(1)} all-to-all(bf16[32,80,128]{2,1,0:T(8,128)(2,1)S(1)} %back.1), channel_id=1, replica_groups=mesh['leaf'=8,'sub'=4] {'leaf','sub'}, dimensions={0} | all-to-all | bytes 1310720 | tf_op jit(solution)/shard_map/all_to_all | solution.py:463
  80.4 5.3 %final.1 = bf16[64,5120]{1,0:T(8,128)(2,1)} custom-call(bf16[32,80,128]{2,1,0:T(8,128)(2,1)S(1)} %all_to_all.11.ret_ref, s32[40,128]{1,0:T(8,128)S(1)} %get-tuple-element.25.row_ref, s32[40,128]{1,0:T(8,128)S(1)} %get-tuple-element.26.part_ref), custom_call_target="tpu_custom_call" | custom-call | flops 1073741824 | bytes 1048576 | tf_op jit(solution)/shard_map/final/pallas_call | solution.py:533
Async XLA Ops:
  32.5 22.4 %copy-start = (bf16[9,32,4096]{2,1,0:T(8,128)(2,1)S(1)}, bf16[9,32,4096]{2,1,0:T(8,128)(2,1)}, u32[]{:S(2)}) copy-start(bf16[9,32,4096]{2,1,0:T(8,128)(2,1)} %left.1) | copy-start | bytes 7077892
  39.6 1.3 %collective-permute-start = (bf16[160,128]{1,0:T(8,128)(2,1)S(1)}, bf16[160,128]{1,0:T(8,128)(2,1)S(1)}, u32[]{:S(2)}, u32[]{:S(2)}) collective-permute-start(bf16[160,128]{1,0:T(8,128)(2,1)S(1)} %get-tuple-element.20.refs_0_), channel_id=1, source_target_pairs={{0,1},{1,0},{2,3},{3,2},{4,5},{5,4},{6,7},{7,6},{8,9},{9,8},{10,11... | collective-permute-start | bytes 122888 | tf_op jit(solution)/shard_map/ppermute | solution.py:409
  41.2 4.9 %collective-permute-start.3 = (bf16[128,128]{1,0:T(8,128)(2,1)S(1)}, bf16[128,128]{1,0:T(8,128)(2,1)S(1)}, u32[]{:S(2)}, u32[]{:S(2)}) collective-permute-start(bf16[128,128]{1,0:T(8,128)(2,1)S(1)} %get-tuple-element.22.refs_0_), channel_id=1, source_target_pairs={{0,6},{1,7},{2,4},{3,5},{4,2},{5,3},{6,0},{7,1},{8,14},{9,15},{10,... | collective-permute-start | bytes 98312 | tf_op jit(solution)/shard_map/ppermute | solution.py:409
  43.6 3.9 %collective-permute-start.2 = (bf16[128,128]{1,0:T(8,128)(2,1)S(1)}, bf16[128,128]{1,0:T(8,128)(2,1)S(1)}, u32[]{:S(2)}, u32[]{:S(2)}) collective-permute-start(bf16[128,128]{1,0:T(8,128)(2,1)S(1)} %get-tuple-element.22.refs_0_), channel_id=1, source_target_pairs={{0,4},{1,5},{2,6},{3,7},{4,0},{5,1},{6,2},{7,3},{8,12},{9,13},{10,... | collective-permute-start | bytes 98312 | tf_op jit(solution)/shard_map/ppermute | solution.py:409
  44.2 3.9 %collective-permute-start.1 = (bf16[128,128]{1,0:T(8,128)(2,1)S(1)}, bf16[128,128]{1,0:T(8,128)(2,1)S(1)}, u32[]{:S(2)}, u32[]{:S(2)}) collective-permute-start(bf16[128,128]{1,0:T(8,128)(2,1)S(1)} %get-tuple-element.22.refs_0_), channel_id=1, source_target_pairs={{0,2},{1,3},{2,0},{3,1},{4,6},{5,7},{6,4},{7,5},{8,10},{9,11},{10,... | collective-permute-start | bytes 98312 | tf_op jit(solution)/shard_map/ppermute | solution.py:409
  48.6 5.6 %collective-permute-start.6 = (bf16[64,128]{1,0:T(8,128)(2,1)S(1)}, bf16[64,128]{1,0:T(8,128)(2,1)S(1)}, u32[]{:S(2)}, u32[]{:S(2)}) collective-permute-start(bf16[64,128]{1,0:T(8,128)(2,1)S(1)} %get-tuple-element.24.refs_2_), channel_id=1, source_target_pairs={{0,24},{1,25},{2,26},{3,27},{4,28},{5,29},{6,30},{7,31},{8,16},{9,... | collective-permute-start | bytes 49160 | tf_op jit(solution)/shard_map/ppermute | solution.py:409
  50.1 4.6 %collective-permute-start.5 = (bf16[64,128]{1,0:T(8,128)(2,1)S(1)}, bf16[64,128]{1,0:T(8,128)(2,1)S(1)}, u32[]{:S(2)}, u32[]{:S(2)}) collective-permute-start(bf16[64,128]{1,0:T(8,128)(2,1)S(1)} %get-tuple-element.24.refs_2_), channel_id=1, source_target_pairs={{0,16},{1,17},{2,18},{3,19},{4,20},{5,21},{6,22},{7,23},{8,24},{9,... | collective-permute-start | bytes 49160 | tf_op jit(solution)/shard_map/ppermute | solution.py:409
  50.8 4.1 %collective-permute-start.4 = (bf16[64,128]{1,0:T(8,128)(2,1)S(1)}, bf16[64,128]{1,0:T(8,128)(2,1)S(1)}, u32[]{:S(2)}, u32[]{:S(2)}) collective-permute-start(bf16[64,128]{1,0:T(8,128)(2,1)S(1)} %get-tuple-element.24.refs_2_), channel_id=1, source_target_pairs={{0,8},{1,9},{2,10},{3,11},{4,12},{5,13},{6,14},{7,15},{8,0},{9,1},... | collective-permute-start | bytes 49160 | tf_op jit(solution)/shard_map/ppermute | solution.py:409
